TPU v7x, 128 devices: a whole 4x4x4 slice. The times are simulated.
128 devices in a mesh: ep: 32 (over y, x, core), tp: 4 (over z).
Axes of the slice: x: 4, y: 4, z: 4, core: 2. Of those that a mesh axis runs over, the one named last changes fastest.
Arguments:
- tokens: bfloat16 [8192, 7168], P('ep', 'tp'), may hold values from -78 to 78
- norm_gain: bfloat16 [7168], P('tp'), may hold values from 0.5 to 1.5
- expert_ids: int32 [8192, 8], P('ep'), may hold values from 0 to 255, all different within a row
- gate_prob: bfloat16 [8192, 8], P('ep'), may hold values from 0.049804688 to 1
- w_gate: bfloat16 [32, 7168, 2048], P('ep', None, 'tp'), may hold values from -0.0625 to 0.0625
- w_up: bfloat16 [32, 7168, 2048], P('ep', None, 'tp'), may hold values from -0.0625 to 0.0625
- w_down: bfloat16 [32, 2048, 7168], P('ep', 'tp'), may hold values from -0.125 to 0.125
Outputs:
- combined: bfloat16 [8192, 7168], P('ep', 'tp')
Inputs may be any that keep to these rules, and one draw needn't show every extreme that they name: `expert_ids`: each row names 8 different experts.
All inputs are finite; a program needn't handle non-finite values.
Results may differ from a plain program's by a relative error of at most 0.01.
Values may be sent and summed in bfloat16 or wider, within the bound.
A program may use at most 128 MiB of HBM per device.

v0:
```python
import jax
import jax.numpy as jnp
from jax import lax
from jax.sharding import PartitionSpec as P

D = 7168
TOP = 8
EXP_DEV = 8


epsilon = 1e-06


def from_everyone(value, axis):
    length = lax.axis_size(axis)
    return lax.all_to_all(
        jnp.broadcast_to(value[None], (length, *value.shape)), axis, 0, 0, tiled=True
    )


def over_copies(value, axis):
    everything = from_everyone(value, axis)
    return jnp.sum(everything, axis=0)


def exchange_in_groups(value, axis, split_dim, concat_dim, work, item_dim, out_dim):
    items = jax.tree.leaves(value)[0].shape[item_dim]
    count = 2 if items % 2 == 0 else 1
    done = []
    for k in range(count):
        group = jax.tree.map(
            lambda a: lax.slice_in_dim(
                a, k * (items // count), (k + 1) * (items // count), axis=item_dim
            ),
            value,
        )
        done.append(
            work(
                lax.all_to_all(
                    group, axis, split_axis=split_dim, concat_axis=concat_dim, tiled=True
                )
            )
        )
    return jax.tree.map(lambda *parts: jnp.concatenate(parts, axis=out_dim), *done)


def place_picks(expert_ids, gate_prob, window, capacity):
    is_live = expert_ids < window
    matches = (expert_ids[:, :, None] == jnp.arange(window, dtype=jnp.int32)).astype(jnp.int32)
    counts = jnp.sum(matches, axis=1)
    before = jnp.cumsum(counts, axis=0) - counts
    slot_index = jnp.sum(matches * before[:, None, :], axis=2)
    is_kept = is_live & (slot_index < capacity)
    target = jnp.where(is_kept, expert_ids * capacity + slot_index, -1)
    hit_table = target[:, :, None] == jnp.arange(window * capacity, dtype=jnp.int32)
    dispatch_mat = jnp.any(hit_table, axis=1).astype(jnp.bfloat16)
    weight_mat = jnp.sum(
        jnp.where(hit_table, gate_prob.astype(jnp.float32)[:, :, None], 0.0), axis=1
    ).astype(jnp.bfloat16)
    return (dispatch_mat, weight_mat)


def run_expert(received, w_gate, w_up, w_down):
    senders, item_count, row_width = received.shape
    flat_rows = received.reshape(senders * item_count, row_width)
    gate_act = jnp.dot(flat_rows, w_gate[0], preferred_element_type=jnp.float32)
    up_act = jnp.dot(flat_rows, w_up[0], preferred_element_type=jnp.float32)
    hidden = (jax.nn.silu(gate_act) * up_act).astype(jnp.bfloat16)
    down_term = jnp.einsum("rf,fc->rc", hidden, w_down[0], preferred_element_type=jnp.float32)
    summed = lax.psum_scatter(down_term.astype(jnp.bfloat16), "tp", scatter_dimension=1, tiled=True)
    shares = summed.reshape(senders, item_count, -1)
    return lax.all_to_all(shares, "ep", split_axis=0, concat_axis=0, tiled=True)


def local(tokens, norm_gain, expert_ids, gate_prob, w_gate, w_up, w_down):
    window = lax.axis_size("ep")
    tok_rows = tokens.shape[0]
    capacity = max(2, 2 * tok_rows * TOP // (EXP_DEV * window))
    dispatch_mat, weight_mat = place_picks(expert_ids, gate_prob, window, capacity)
    values = tokens.astype(jnp.float32)
    square_part = jnp.sum(values * values, axis=1)
    square_total = over_copies(square_part, "tp")
    inverse_rms = lax.rsqrt(square_total / D + epsilon)
    normed = (values * inverse_rms[:, None] * norm_gain.astype(jnp.float32)).astype(jnp.bfloat16)
    outgoing = jnp.einsum("tp,td->pd", dispatch_mat, normed, preferred_element_type=jnp.float32)
    outgoing = outgoing.astype(jnp.bfloat16).reshape(window, capacity, -1)

    def handle(received):
        gathered = lax.all_gather(received, "tp", axis=2, tiled=True)
        return run_expert(gathered, w_gate, w_up, w_down)

    returned = exchange_in_groups(outgoing, "ep", 0, 0, handle, 1, 1)
    flat_back = returned.reshape(-1, returned.shape[2])
    combined = jnp.einsum("tp,pd->td", weight_mat, flat_back, preferred_element_type=jnp.float32)
    return combined.astype(jnp.bfloat16)


def solution(mesh):
    placed = (
        P("ep", "tp"),
        P("tp"),
        P("ep", None),
        P("ep", None),
        P("ep", None, "tp"),
        P("ep", None, "tp"),
        P("ep", "tp", None),
    )
    return jax.shard_map(
        local, mesh=mesh, in_specs=placed, out_specs=P("ep", "tp"), check_vma=False
    )
```

profile of v0, /device:TPU:1, one launch (start us, length us, event | category | flops | bytes accessed | tf_op | source)
XLA Modules:
  0.0 255.4 jit_solution(9727998538408173753)
XLA Ops:
  6.5 1.4 fusion.15
  8.0 0.6 broadcast_in_dim.21
  8.6 5.8 %all-to-all-start = ((f32[4,1,256]{2,1,0:T(1,128)}), f32[4,1,256]{2,1,0:T(1,128)S(1)}, u32[]{:S(2)}, u32[]{:S(2)}) async-start(f32[4,1,256]{2,1,0:T(1,128)} %broadcast_in_dim.21), calls=%async_computation | async-start | bytes 8192 | tf_op jit(solution)/shard_map/all_to_all | solution.py:16
  14.4 0.0 all-gather.3.cloned.1.call-start
  14.4 0.7 convert_reduce_fusion
  15.2 0.6 reduce-window.6
  15.8 0.2 slice_reduce_fusion
  16.0 0.1 fusion.52
  16.1 0.8 select_reduce_fusion.1
  16.8 0.7 add_select_fusion
  17.5 0.1 copy.23
  17.7 1.7 fusion.10
  19.4 0.7 convert_element_type.41
  20.1 0.0 all-to-all-done
  20.1 2.0 convolution_convert_fusion.2
  22.1 0.1 fusion.55
  22.3 23.6 %all_to_all.26 = bf16[32,8,1792]{2,1,0:T(8,128)(2,1)} all-to-all(bf16[32,8,1792]{2,1,0:T(8,128)(2,1)S(1)} %get-tuple-element.5), channel_id=1, replica_groups=mesh['ep'=32,'tp'=4] {'ep'}, dimensions={0} | all-to-all | bytes 1835008 | tf_op jit(solution)/shard_map/all_to_all | solution.py:39
  45.9 0.0 all-gather.3.cloned.1.call-update
  45.9 0.0 all-gather.5.cloned.1.call-start
  45.9 19.5 %all_to_all.27 = bf16[32,8,1792]{2,1,0:T(8,128)(2,1)} all-to-all(bf16[32,8,1792]{2,1,0:T(8,128)(2,1)S(1)} %get-tuple-element.6), channel_id=1, replica_groups=mesh['ep'=32,'tp'=4] {'ep'}, dimensions={0} | all-to-all | bytes 1835008 | tf_op jit(solution)/shard_map/all_to_all | solution.py:39
  65.4 0.0 all-gather.5.cloned.1.call-update
  65.5 0.0 reduce-scatter.3.cloned.1.call-start
  65.5 22.4 %all-gather.3.cloned.1.call-done = bf16[32,8,7168]{2,1,0:T(8,128)(2,1)} async-done(((bf16[32,8,1792]{2,1,0:T(8,128)(2,1)}), bf16[32,8,7168]{2,1,0:T(8,128)(2,1)}) %all-gather.3.cloned.1.call-update) | async-done | bytes 3670032 | tf_op jit(solution)/shard_map/all_gather | solution.py:89
  87.9 6.2 %fusion.8 = f32[256,512]{1,0:T(8,128)S(1)} fusion(bf16[1,7168,512]{2,1,0:T(8,128)(2,1)} %param.11, bf16[32,8,7168]{2,1,0:T(8,128)(2,1)} %all-gather.3.cloned.1.call-done), kind=kOutput, calls=%fused_computation.10 | convolution fusion | flops 1879048192 | bytes 11534336 | tf_op jit(solution)/shard_map/dot_general | solution.py:66
  94.1 12.6 %convolution_convert_fusion.1 = bf16[256,7168]{1,0:T(8,128)(2,1)} fusion(bf16[1,512,7168]{2,1,0:T(8,128)(2,1)} %param.13, bf16[1,7168,512]{2,1,0:T(8,128)(2,1)} %param.12, bf16[32,8,7168]{2,1,0:T(8,128)(2,1)} %all-gather.3.cloned.1.call-done, f32[256,512]{1,0:T(8,128)S(1)} %fusion.8), kind=kOutput, calls=%fused_computation.1 | convolution fusion | flops 3760717824 | bytes 22544384 | tf_op jit(solution)/shard_map/rf,fc->rc/dot_general | solution.py:69
  106.8 0.0 reduce-scatter.3.cloned.1.call-update
  106.8 0.2 reduce-scatter.5.cloned.1.call-start
  107.0 26.7 %all-gather.5.cloned.1.call-done = bf16[32,8,7168]{2,1,0:T(8,128)(2,1)} async-done(((bf16[32,8,1792]{2,1,0:T(8,128)(2,1)}), bf16[32,8,7168]{2,1,0:T(8,128)(2,1)}) %all-gather.5.cloned.1.call-update) | async-done | bytes 3670032 | tf_op jit(solution)/shard_map/all_gather | solution.py:89
  133.8 6.2 %fusion.6 = f32[256,512]{1,0:T(8,128)S(1)} fusion(bf16[1,7168,512]{2,1,0:T(8,128)(2,1)} %param.11, bf16[32,8,7168]{2,1,0:T(8,128)(2,1)} %all-gather.5.cloned.1.call-done), kind=kOutput, calls=%fused_computation.8 | convolution fusion | flops 1879048192 | bytes 11534336 | tf_op jit(solution)/shard_map/dot_general | solution.py:66
  140.0 12.8 %convolution_convert_fusion = bf16[256,7168]{1,0:T(8,128)(2,1)} fusion(bf16[1,512,7168]{2,1,0:T(8,128)(2,1)} %param.13, bf16[1,7168,512]{2,1,0:T(8,128)(2,1)} %param.12, bf16[32,8,7168]{2,1,0:T(8,128)(2,1)} %all-gather.5.cloned.1.call-done, f32[256,512]{1,0:T(8,128)S(1)} %fusion.6), kind=kOutput, calls=%fused_computation | convolution fusion | flops 3760717824 | bytes 22544384 | tf_op jit(solution)/shard_map/rf,fc->rc/dot_general | solution.py:69
  152.8 0.0 copy-start
  152.8 0.0 reduce-scatter.5.cloned.1.call-update
  152.9 26.3 %reduce-scatter.3.cloned.1.call-done = bf16[256,1792]{1,0:T(8,128)(2,1)} async-done(((bf16[256,7168]{1,0:T(8,128)(2,1)}), bf16[256,1792]{1,0:T(8,128)(2,1)}) %reduce-scatter.3.cloned.1.call-update) | async-done | bytes 917520 | tf_op jit(solution)/shard_map/reduce_scatter | solution.py:70
  179.2 7.6 %all-to-all-start.2 = ((bf16[32,8,1792]{2,1,0:T(8,128)(2,1)}), bf16[32,8,1792]{2,1,0:T(8,128)(2,1)S(1)}, u32[]{:S(2)}, u32[]{:S(2)}) async-start(bf16[32,8,1792]{2,1,0:T(8,128)(2,1)} %bitcast.75), calls=%async_computation.3 | async-start | bytes 1835008 | tf_op jit(solution)/shard_map/all_to_all | solution.py:72
  186.8 37.1 %reduce-scatter.5.cloned.1.call-done = bf16[256,1792]{1,0:T(8,128)(2,1)} async-done(((bf16[256,7168]{1,0:T(8,128)(2,1)}), bf16[256,1792]{1,0:T(8,128)(2,1)}) %reduce-scatter.5.cloned.1.call-update) | async-done | bytes 917520 | tf_op jit(solution)/shard_map/reduce_scatter | solution.py:70
  223.9 0.0 all-to-all-done.2
  223.9 7.6 %all-to-all-start.4 = ((bf16[32,8,1792]{2,1,0:T(8,128)(2,1)}), bf16[32,8,1792]{2,1,0:T(8,128)(2,1)S(1)}, u32[]{:S(2)}, u32[]{:S(2)}) async-start(bf16[32,8,1792]{2,1,0:T(8,128)(2,1)} %bitcast.76), calls=%async_computation.6 | async-start | bytes 1835008 | tf_op jit(solution)/shard_map/all_to_all | solution.py:72
  231.5 0.0 copy-done
  231.5 0.1 copy.24
  231.6 1.7 select_reduce_fusion
  233.3 13.8 %all-to-all-done.4 = bf16[32,8,1792]{2,1,0:T(8,128)(2,1)S(1)} async-done(((bf16[32,8,1792]{2,1,0:T(8,128)(2,1)}), bf16[32,8,1792]{2,1,0:T(8,128)(2,1)S(1)}, u32[]{:S(2)}, u32[]{:S(2)}) %all-to-all-start.4) | async-done | bytes 917536 | tf_op jit(solution)/shard_map/all_to_all | solution.py:72
  247.1 0.1 pad_maximum_fusion
  247.3 1.6 convolution_convert_fusion.3
  (5 shorter events, 0.1 us)
Async XLA Ops:
  8.6 11.5 %all-to-all-start = ((f32[4,1,256]{2,1,0:T(1,128)}), f32[4,1,256]{2,1,0:T(1,128)S(1)}, u32[]{:S(2)}, u32[]{:S(2)}) async-start(f32[4,1,256]{2,1,0:T(1,128)} %broadcast_in_dim.21), calls=%async_computation | async-start | bytes 8192 | tf_op jit(solution)/shard_map/all_to_all | solution.py:16
  14.4 73.5 %all-gather.3.cloned.1.call-start = ((), (), s32[]{:S(2)}) async-start(), calls=%async_computation.7 | async-start | bytes 4587520 | tf_op jit(solution)/shard_map/all_gather | solution.py:89
  45.9 87.9 %all-gather.5.cloned.1.call-start = ((), (), s32[]{:S(2)}) async-start(), calls=%async_computation.9 | async-start | bytes 4587520 | tf_op jit(solution)/shard_map/all_gather | solution.py:89
  65.5 113.8 %reduce-scatter.3.cloned.1.call-start = ((), (), s32[]{:S(2)}) async-start(), calls=%async_computation.8 | async-start | bytes 4587520 | tf_op jit(solution)/shard_map/reduce_scatter | solution.py:70
  106.8 117.1 %reduce-scatter.5.cloned.1.call-start = ((), (), s32[]{:S(2)}) async-start(), calls=%async_computation.10 | async-start | bytes 4587520 | tf_op jit(solution)/shard_map/reduce_scatter | solution.py:70
  152.8 78.6 %copy-start = (bf16[256,8]{0,1:T(8,128)(2,1)S(1)}, bf16[256,8]{0,1:T(8,128)(2,1)}, u32[]{:S(2)}) copy-start(bf16[256,8]{0,1:T(8,128)(2,1)} %param.10) | copy-start | bytes 12292
  179.2 44.7 %all-to-all-start.2 = ((bf16[32,8,1792]{2,1,0:T(8,128)(2,1)}), bf16[32,8,1792]{2,1,0:T(8,128)(2,1)S(1)}, u32[]{:S(2)}, u32[]{:S(2)}) async-start(bf16[32,8,1792]{2,1,0:T(8,128)(2,1)} %bitcast.75), calls=%async_computation.3 | async-start | bytes 1835008 | tf_op jit(solution)/shard_map/all_to_all | solution.py:72
  223.9 23.2 %all-to-all-start.4 = ((bf16[32,8,1792]{2,1,0:T(8,128)(2,1)}), bf16[32,8,1792]{2,1,0:T(8,128)(2,1)S(1)}, u32[]{:S(2)}, u32[]{:S(2)}) async-start(bf16[32,8,1792]{2,1,0:T(8,128)(2,1)} %bitcast.76), calls=%async_computation.6 | async-start | bytes 1835008 | tf_op jit(solution)/shard_map/all_to_all | solution.py:72
Sparse Core Ops, SparseCore 0:
  46.0 41.8 all-gather.2
  89.6 44.1 all-gather.4
  136.2 42.9 reduce-scatter.2
  181.5 42.3 reduce-scatter.4
where the time goes:
time: 256 us; the launch traced here: 255 us
  waiting for transfers between devices  126 us (49%)
  blocking collectives  43.1 us (17%)
  matrix products  41.6 us (16%)
  starting transfers between devices  21.3 us (8%)
  between operations  13.2 us (5%)
  other arithmetic  8.58 us (3%)
    reduce_scatter x2, waiting for transfers between devices, run_expert(): lax.psum_scatter(down_term.astype(jnp.bfloat16), 'tp', scatter_dimension=...  63.4 us
    all_gather x2, waiting for transfers between devices, handle(): gathered = lax.all_gather(received, 'tp', axis=2, tiled=True)  49.1 us
    all_to_all x2, blocking collectives, exchange_in_groups(): lax.all_to_all(group, axis, split_axis=split_dim, concat_axis=concat_dim,...  43.1 us
    dot_general x2, matrix products, run_expert(): jnp.einsum('rf,fc->rc', hidden, w_down[0], preferred_element_type=jnp.flo...  25.5 us
    all_to_all x2, starting transfers between devices, run_expert(): return lax.all_to_all(shares, 'ep', split_axis=0, concat_axis=0, tiled=True)  15.2 us
    all_to_all x2, waiting for transfers between devices, run_expert(): return lax.all_to_all(shares, 'ep', split_axis=0, concat_axis=0, tiled=True)  13.8 us
    dot_general x2, matrix products, run_expert(): gate_act = jnp.dot(flat_rows, w_gate[0], preferred_element_type=jnp.float32)  12.5 us
    all_to_all x1, starting transfers between devices, from_everyone(): lax.all_to_all(jnp.broadcast_to(value[None], (length, *value.shape)), axi...  5.84 us
  transfers between devices with their start and end apart: 7, of which 5 were waited for; matrix products, arithmetic and copies ran while one was open for 18% of the time, Pallas kernels for 0%

commit v1 on v0

v1 whole, which is shorter than its diff:
```python
import functools

import jax
import jax.numpy as jnp
from jax import lax
from jax.experimental import pallas as pl
from jax.experimental.pallas import tpu as pltpu
from jax.sharding import PartitionSpec as P

MESH = pl.DeviceIdType.MESH
F32 = jnp.float32
BF16 = jnp.bfloat16

D = 7168
CAP = 16
CORES = 2
NZ = 4
CHUNK = 256
ROUTE_A = 4
WEIGHT_PIECES = 4
epsilon = 1e-06


def moe_kernel(
    cfg,
    tokens_ref,
    gain_ref,
    ids_ref,
    prob_ref,
    wg_hbm,
    wu_hbm,
    wd_hbm,
    out_ref,
    wg,
    wu,
    wd,
    sq_buf,
    disp_t,
    comb,
    xa,
    xb,
    nb,
    out_a,
    out_b,
    acc_g,
    acc_u,
    hid,
    far_a,
    far_in_a,
    near_a,
    near_in_a,
    ret_a,
    ret_b,
    far_b,
    far_in_b,
    near_b,
    near_in_b,
    w_sem,
    sq_send,
    sq_recv,
    da_send,
    da_recv,
    db_send,
    db_recv,
    za_send,
    za_recv,
    zb_send,
    zb_recv,
    ra_send,
    ra_recv,
    rb_send,
    rb_recv,
    ya_send,
    ya_recv,
    yb_send,
    yb_recv,
):
    E, NA, NB, CW, FFD = cfg["E"], cfg["NA"], cfg["NB"], cfg["CW"], cfg["FFD"]
    DZ, T = cfg["DZ"], cfg["T"]
    S = E * CAP
    EH = E // 2
    SH = S // 2
    TH = T // 2
    e = lax.axis_index("ep")
    z = lax.axis_index("tp")
    zp = lax.rem(z + 1, NZ)
    zm = lax.rem(z + 3, NZ)
    zf = lax.rem(z + 2, NZ)

    def peer_of(k):
        off = lax.rem(k * cfg["STRIDE"], E)
        chip = lax.rem(e // CORES + off // CORES, E // CORES)
        if cfg["NX"] > 1:
            nx = cfg["NX"]
            oc = off // CORES
            mc = e // CORES
            py = lax.rem(mc // nx + oc // nx, E // CORES // nx)
            px = lax.rem(lax.rem(mc, nx) + lax.rem(oc, nx), nx)
            chip = py * nx + px
        core = lax.rem(lax.rem(e, CORES) + lax.rem(off, CORES), CORES)
        return chip * CORES + core

    def to_z(src, dst, send, recv, zt):
        return pltpu.make_async_remote_copy(
            src_ref=src, dst_ref=dst, send_sem=send, recv_sem=recv, device_id=(e, zt), device_id_type=MESH
        )

    def to_e(src, dst, send, recv, et):
        return pltpu.make_async_remote_copy(
            src_ref=src, dst_ref=dst, send_sem=send, recv_sem=recv, device_id=(et, z), device_id_type=MESH
        )

    def take(ref, sem):
        pltpu.make_async_copy(ref, ref, sem).wait()

    rows_w = wg.shape[0] // WEIGHT_PIECES
    rows_d = wd.shape[0] // WEIGHT_PIECES
    weight_copies = []
    for p in range(WEIGHT_PIECES):
        rs = pl.ds(p * rows_w, rows_w)
        weight_copies.append(pltpu.make_async_copy(wg_hbm.at[rs], wg.at[rs], w_sem.at[0, p]))
        weight_copies.append(pltpu.make_async_copy(wu_hbm.at[rs], wu.at[rs], w_sem.at[1, p]))
    down_copies = []
    for p in range(WEIGHT_PIECES):
        rs = pl.ds(p * rows_d, rows_d)
        down_copies.append(pltpu.make_async_copy(wd_hbm.at[rs], wd.at[rs], w_sem.at[2, p]))

    barrier = pltpu.get_barrier_semaphore()

    def greet(k, carry):
        pl.semaphore_signal(barrier, inc=1, device_id=(peer_of(k), z), device_id_type=MESH)
        return carry

    lax.fori_loop(1, E, greet, 0)
    for dz in range(1, NZ):
        pl.semaphore_signal(barrier, inc=1, device_id=(e, lax.rem(z + dz, NZ)), device_id_type=MESH)
    for copy in weight_copies + down_copies:
        copy.start()

    values = tokens_ref[...].astype(F32)
    part = jnp.sum(values * values, axis=1, keepdims=True)
    if T < 128:
        part = jnp.concatenate([part, jnp.zeros((128 - T, 1), F32)], axis=0)
    TP = max(T, 128)
    part_t = jnp.transpose(jnp.broadcast_to(part, (TP, 128)))
    sq_buf[z] = part_t[0:8, :]
    pl.semaphore_wait(barrier, E - 1 + NZ - 1)
    sq_copies = []
    for dz in range(1, NZ):
        copy = to_z(sq_buf.at[z], sq_buf.at[z], sq_send.at[dz - 1], sq_recv.at[dz - 1], lax.rem(z + dz, NZ))
        copy.start()
        sq_copies.append(copy)

    ids = ids_ref[...]
    probs = prob_ref[...].astype(F32)
    expert_iota = lax.broadcasted_iota(jnp.int32, (T, E), 1)
    match = jnp.zeros((T, E), F32)
    weight = jnp.zeros((T, E), F32)
    for k in range(ids.shape[1]):
        hit = ids[:, k : k + 1] == expert_iota
        match = match + jnp.where(hit, 1.0, 0.0)
        weight = weight + jnp.where(hit, probs[:, k : k + 1], 0.0)
    lower = jnp.where(
        lax.broadcasted_iota(jnp.int32, (T, T), 0) > lax.broadcasted_iota(jnp.int32, (T, T), 1), 1.0, 0.0
    ).astype(BF16)
    match_b = match.astype(BF16)
    before = jnp.dot(lower, match_b, preferred_element_type=F32).astype(BF16)
    spread_row = lax.broadcasted_iota(jnp.int32, (E, S), 0)
    spread_col = lax.broadcasted_iota(jnp.int32, (E, S), 1)
    spread = jnp.where(spread_col // CAP == spread_row, 1.0, 0.0).astype(BF16)
    match_s = jnp.dot(match_b, spread, preferred_element_type=F32)
    before_s = jnp.dot(before, spread, preferred_element_type=F32)
    weight_s = jnp.dot(weight.astype(BF16), spread, preferred_element_type=F32)
    slot_of = lax.rem(lax.broadcasted_iota(jnp.int32, (T, S), 1), CAP).astype(F32)
    chosen = jnp.where((match_s > 0.5) & (before_s == slot_of), 1.0, 0.0)
    comb[...] = (chosen * weight_s).astype(BF16)
    disp_t[...] = jnp.transpose(chosen).astype(BF16)
    acc_g[...] = jnp.zeros_like(acc_g)
    acc_u[...] = jnp.zeros_like(acc_u)

    for copy in sq_copies:
        copy.wait()
    total_t = sq_buf[0] + sq_buf[1] + sq_buf[2] + sq_buf[3]
    total = jnp.transpose(jnp.broadcast_to(total_t[0:1, :], (128, TP)))[0:T, 0:1]
    inverse = lax.rsqrt(total / cfg["D"] + epsilon)

    def cols(c):
        return pl.ds(pl.multiple_of(c * CW, CW), CW)

    def normed(c):
        v = tokens_ref[:, cols(c)].astype(F32)
        return (v * inverse * gain_ref[:, cols(c)].astype(F32)).astype(BF16)

    for c in range(NB):
        nb[c, z] = normed(NA + c)
        for i, zt in ((0, zp), (1, zm)):
            to_z(nb.at[c, z], nb.at[c, z], zb_send.at[i, c], zb_recv.at[i, c], zt).start()

    for c in range(NA):
        rows = jnp.dot(disp_t[...], normed(c), preferred_element_type=F32).astype(BF16)
        out_a[c] = rows.reshape(E, CAP, CW)
        xa[c, z, e] = out_a[c, e]

        def send_a(k, carry, c=c):
            et = peer_of(k)
            to_e(out_a.at[c, et], xa.at[c, z, e], da_send.at[c], da_recv.at[c], et).start()
            return carry

        lax.fori_loop(1, E, send_a, 0)

    def forward_b(c):
        take(nb.at[c, zm], zb_recv.at[0, c])
        lo, hi = pl.ds(0, TH), pl.ds(TH, TH)
        to_z(nb.at[c, zm, lo], nb.at[c, zm, lo], zb_send.at[2, c], zb_recv.at[2, c], zp).start()
        take(nb.at[c, zp], zb_recv.at[1, c])
        to_z(nb.at[c, zp, hi], nb.at[c, zp, hi], zb_send.at[3, c], zb_recv.at[3, c], zm).start()

    def dispatch_b(c):
        take(nb.at[c, zf, pl.ds(0, TH)], zb_recv.at[2, c])
        take(nb.at[c, zf, pl.ds(TH, TH)], zb_recv.at[3, c])
        for q in range(NZ):
            rows = jnp.dot(disp_t[...], nb[c, q], preferred_element_type=F32).astype(BF16)
            out_b[c, :, q] = rows.reshape(E, CAP, CW)
        xb[c, e] = out_b[c, e]

        def send_b(k, carry):
            et = peer_of(k)
            to_e(out_b.at[c, et], xb.at[c, e], db_send.at[c], db_recv.at[c], et).start()
            return carry

        lax.fori_loop(1, E, send_b, 0)

    def direct_a(c):
        take(xa.at[c, z, pl.ds(0, E - 1)], da_recv.at[c])
        for i, zt in ((0, zp), (1, zm)):
            to_z(xa.at[c, z], xa.at[c, z], za_send.at[i, c], za_recv.at[i, c], zt).start()

    def forward_a(c):
        lo, hi = pl.ds(0, EH), pl.ds(EH, EH)
        take(xa.at[c, zm], za_recv.at[0, c])
        to_z(xa.at[c, zm, lo], xa.at[c, zm, lo], za_send.at[2, c], za_recv.at[2, c], zp).start()
        take(xa.at[c, zp], za_recv.at[1, c])
        to_z(xa.at[c, zp, hi], xa.at[c, zp, hi], za_send.at[3, c], za_recv.at[3, c], zm).start()

    def multiply(blocks, base):
        x = jnp.concatenate([b.reshape(S, CW) for b in blocks], axis=1)
        for w_ref, acc in ((wg, acc_g), (wu, acc_u)):
            w = jnp.concatenate(
                [w_ref[pl.ds(pl.multiple_of(q * DZ + base, CW), CW), :] for q in range(NZ)], axis=0
            )
            acc[...] += jnp.dot(x, w, preferred_element_type=F32)

    def matmul_a(c):
        take(xa.at[c, zf, pl.ds(0, EH)], za_recv.at[2, c])
        take(xa.at[c, zf, pl.ds(EH, EH)], za_recv.at[3, c])
        multiply([xa[c, q] for q in range(NZ)], c * CW)

    def matmul_b(c):
        take(xb.at[c, pl.ds(0, E - 1)], db_recv.at[c])
        multiply([xb[c, :, q] for q in range(NZ)], (NA + c) * CW)

    def wait_weights():
        for copy in weight_copies:
            copy.wait()

    def run(steps, count):
        def body(it, carry):
            for fn, first, n in steps:
                if n > 0:

                    @pl.when((it >= first) & (it < first + n))
                    def _(fn=fn, first=first):
                        fn(it - first)

            return carry

        lax.fori_loop(0, count, body, 0)

    wait_weights()
    run(
        (
            (forward_b, 0, NB),
            (direct_a, 0, NA),
            (dispatch_b, 1, NB),
            (forward_a, 1, NA),
            (matmul_a, 2, NA),
            (matmul_b, NB + 1, NB),
        ),
        max(NA + 2, 2 * NB + 1),
    )

    g = acc_g[...]
    hid[...] = (g / (1.0 + jnp.exp(-g)) * acc_u[...]).astype(BF16)
    for copy in down_copies:
        copy.wait()

    def down(q, c):
        ds = pl.ds(pl.multiple_of(q * DZ + c * CW, CW), CW)
        return jnp.dot(hid[...], wd[:, ds], preferred_element_type=F32).astype(BF16)

    lo_s, hi_s = pl.ds(0, SH), pl.ds(SH, SH)

    def far_part_a(c):
        far_a[c] = down(zf, c)
        to_z(far_a.at[c, lo_s], far_in_a.at[c, lo_s], ra_send.at[0, c], ra_recv.at[0, c], zp).start()
        to_z(far_a.at[c, hi_s], far_in_a.at[c, hi_s], ra_send.at[1, c], ra_recv.at[1, c], zm).start()

    def plus(a, b):
        return (a.astype(F32) + b.astype(F32)).astype(BF16)

    def near_part_a(c):
        near_a[c, 0] = down(zp, c)
        near_a[c, 1] = down(zm, c)
        take(far_in_a.at[c, lo_s], ra_recv.at[0, c])
        near_a[c, 0, lo_s] = plus(near_a[c, 0, lo_s], far_in_a[c, lo_s])
        to_z(near_a.at[c, 0], near_in_a.at[c, 0], ra_send.at[2, c], ra_recv.at[2, c], zp).start()
        take(far_in_a.at[c, hi_s], ra_recv.at[1, c])
        near_a[c, 1, hi_s] = plus(near_a[c, 1, hi_s], far_in_a[c, hi_s])
        to_z(near_a.at[c, 1], near_in_a.at[c, 1], ra_send.at[3, c], ra_recv.at[3, c], zm).start()

    def own_part_a(c):
        own = jnp.dot(
            hid[...], wd[:, pl.ds(pl.multiple_of(z * DZ + c * CW, CW), CW)], preferred_element_type=F32
        )
        own = own.astype(BF16).astype(F32)
        take(near_in_a.at[c, 0], ra_recv.at[2, c])
        take(near_in_a.at[c, 1], ra_recv.at[3, c])
        own = own + near_in_a[c, 0].astype(F32) + near_in_a[c, 1].astype(F32)
        out_a[c] = own.astype(BF16).reshape(E, CAP, CW)
        ret_a[c, e] = out_a[c, e]

        def send_back(k, carry):
            et = peer_of(k)
            to_e(out_a.at[c, et], ret_a.at[c, e], ya_send.at[c], ya_recv.at[c], et).start()
            return carry

        lax.fori_loop(1, E, send_back, 0)

    def part_b(c):
        for q in range(NZ):
            out_b[c, :, q] = down(q, NA + c).reshape(E, CAP, CW)
        ret_b[c, e] = out_b[c, e]

        def send_back(k, carry):
            et = peer_of(k)
            to_e(out_b.at[c, et], ret_b.at[c, e], yb_send.at[c], yb_recv.at[c], et).start()
            return carry

        lax.fori_loop(1, E, send_back, 0)

    def weigh_b(c, q):
        return jnp.dot(comb[...], ret_b[c, :, q].reshape(S, CW), preferred_element_type=F32).astype(BF16)

    lo_t, hi_t = pl.ds(0, TH), pl.ds(TH, TH)

    def far_part_b(c):
        take(ret_b.at[c, pl.ds(0, E - 1)], yb_recv.at[c])
        far_b[c] = weigh_b(c, zf)
        to_z(far_b.at[c, lo_t], far_in_b.at[c, lo_t], rb_send.at[0, c], rb_recv.at[0, c], zp).start()
        to_z(far_b.at[c, hi_t], far_in_b.at[c, hi_t], rb_send.at[1, c], rb_recv.at[1, c], zm).start()

    def near_part_b(c):
        near_b[c, 0] = weigh_b(c, zp)
        near_b[c, 1] = weigh_b(c, zm)
        take(far_in_b.at[c, lo_t], rb_recv.at[0, c])
        near_b[c, 0, lo_t] = plus(near_b[c, 0, lo_t], far_in_b[c, lo_t])
        to_z(near_b.at[c, 0], near_in_b.at[c, 0], rb_send.at[2, c], rb_recv.at[2, c], zp).start()
        take(far_in_b.at[c, hi_t], rb_recv.at[1, c])
        near_b[c, 1, hi_t] = plus(near_b[c, 1, hi_t], far_in_b[c, hi_t])
        to_z(near_b.at[c, 1], near_in_b.at[c, 1], rb_send.at[3, c], rb_recv.at[3, c], zm).start()

    def own_part_b(c):
        own = jnp.dot(comb[...], ret_b[c, :, z].reshape(S, CW), preferred_element_type=F32)
        take(near_in_b.at[c, 0], rb_recv.at[2, c])
        take(near_in_b.at[c, 1], rb_recv.at[3, c])
        own = own + near_in_b[c, 0].astype(F32) + near_in_b[c, 1].astype(F32)
        out_ref[:, cols(NA + c)] = own.astype(BF16)

    def combine_a(c):
        take(ret_a.at[c, pl.ds(0, E - 1)], ya_recv.at[c])
        got = jnp.dot(comb[...], ret_a[c].reshape(S, CW), preferred_element_type=F32)
        out_ref[:, cols(c)] = got.astype(BF16)

    def left(ref, sem):
        pltpu.make_async_copy(ref, ref, sem).wait()

    for c in range(NA):
        left(out_a.at[c, pl.ds(0, E - 1)], da_send.at[c])
    for c in range(NB):
        left(out_b.at[c, pl.ds(0, E - 1)], db_send.at[c])

    run(
        (
            (far_part_a, 0, NA),
            (part_b, 0, NB),
            (near_part_a, 1, NA),
            (own_part_a, 2, NA),
            (far_part_b, 3, NB),
            (near_part_b, 4, NB),
        ),
        max(NA + 2, NB + 4),
    )
    for c in range(NA):
        combine_a(c)
    for c in range(NB):
        own_part_b(c)

    for c in range(NA):
        for i in range(2):
            left(xa.at[c, 0], za_send.at[i, c])
            left(xa.at[c, 0, pl.ds(0, EH)], za_send.at[2 + i, c])
            left(far_a.at[c, lo_s], ra_send.at[i, c])
            left(near_a.at[c, 0], ra_send.at[2 + i, c])
        left(out_a.at[c, pl.ds(0, E - 1)], ya_send.at[c])
    for c in range(NB):
        for i in range(2):
            left(nb.at[c, 0], zb_send.at[i, c])
            left(nb.at[c, 0, pl.ds(0, TH)], zb_send.at[2 + i, c])
            left(far_b.at[c, lo_t], rb_send.at[i, c])
            left(near_b.at[c, 0], rb_send.at[2 + i, c])
        left(out_b.at[c, pl.ds(0, E - 1)], yb_send.at[c])


def local(cfg, tokens, norm_gain, expert_ids, gate_prob, w_gate, w_up, w_down):
    E, NA, NB, CW, T = cfg["E"], cfg["NA"], cfg["NB"], cfg["CW"], cfg["T"]
    DZ, FFD = cfg["DZ"], cfg["FFD"]
    S = E * CAP
    a, b = max(NA, 1), max(NB, 1)
    vmem = pl.BlockSpec(memory_space=pltpu.VMEM)
    hbm = pl.BlockSpec(memory_space=pl.ANY)
    TP = max(T, 128)
    dma = pltpu.SemaphoreType.DMA
    scratch = [
        pltpu.VMEM((NZ * DZ, FFD), BF16),
        pltpu.VMEM((NZ * DZ, FFD), BF16),
        pltpu.VMEM((FFD, NZ * DZ), BF16),
        pltpu.VMEM((NZ, 8, TP), F32),
        pltpu.VMEM((S, T), BF16),
        pltpu.VMEM((T, S), BF16),
        pltpu.VMEM((a, NZ, E, CAP, CW), BF16),
        pltpu.VMEM((b, E, NZ, CAP, CW), BF16),
        pltpu.VMEM((b, NZ, T, CW), BF16),
        pltpu.VMEM((a, E, CAP, CW), BF16),
        pltpu.VMEM((b, E, NZ, CAP, CW), BF16),
        pltpu.VMEM((S, FFD), F32),
        pltpu.VMEM((S, FFD), F32),
        pltpu.VMEM((S, FFD), BF16),
        pltpu.VMEM((a, S, CW), BF16),
        pltpu.VMEM((a, S, CW), BF16),
        pltpu.VMEM((a, 2, S, CW), BF16),
        pltpu.VMEM((a, 2, S, CW), BF16),
        pltpu.VMEM((a, E, CAP, CW), BF16),
        pltpu.VMEM((b, E, NZ, CAP, CW), BF16),
        pltpu.VMEM((b, T, CW), BF16),
        pltpu.VMEM((b, T, CW), BF16),
        pltpu.VMEM((b, 2, T, CW), BF16),
        pltpu.VMEM((b, 2, T, CW), BF16),
        dma((3, WEIGHT_PIECES)),
        dma((NZ - 1,)),
        dma((NZ - 1,)),
        dma((a,)),
        dma((a,)),
        dma((b,)),
        dma((b,)),
        dma((4, a)),
        dma((4, a)),
        dma((4, b)),
        dma((4, b)),
        dma((4, a)),
        dma((4, a)),
        dma((4, b)),
        dma((4, b)),
        dma((a,)),
        dma((a,)),
        dma((b,)),
        dma((b,)),
    ]
    return pl.pallas_call(
        functools.partial(moe_kernel, cfg),
        out_shape=jax.ShapeDtypeStruct((T, DZ), BF16),
        in_specs=[vmem, vmem, vmem, vmem, hbm, hbm, hbm],
        out_specs=vmem,
        scratch_shapes=scratch,
        compiler_params=pltpu.CompilerParams(
            collective_id=0, has_side_effects=True, vmem_limit_bytes=cfg["VMEM"]
        ),
        name="moe_layer",
    )(tokens, norm_gain.reshape(1, -1), expert_ids, gate_prob, w_gate[0], w_up[0], w_down[0])


def config(mesh, tokens=8192, width=D, ff=2048, chunk=CHUNK, route_a=ROUTE_A, nx=4):
    E = mesh.shape["ep"]
    DZ = width // NZ
    n = DZ // chunk
    return dict(
        E=E,
        T=tokens // E,
        D=width,
        DZ=DZ,
        FFD=ff // NZ,
        CW=chunk,
        NA=route_a,
        NB=n - route_a,
        NX=nx,
        STRIDE=11,
        VMEM=67_000_000,
    )


def build(mesh, cfg):
    placed = (
        P("ep", "tp"),
        P("tp"),
        P("ep", None),
        P("ep", None),
        P("ep", None, "tp"),
        P("ep", None, "tp"),
        P("ep", "tp", None),
    )
    return jax.shard_map(
        functools.partial(local, cfg), mesh=mesh, in_specs=placed, out_specs=P("ep", "tp"), check_vma=False
    )


def solution(mesh):
    return build(mesh, config(mesh))
```

time: 256 us -> 124 us (0.48)
  waiting for transfers between devices: 126 us -> 0 us
  Pallas kernels: 0 us -> 118 us
  blocking collectives: 43.1 us -> 0 us
  matrix products: 41.6 us -> 0 us
  starting transfers between devices: 21.3 us -> 0 us
  between operations: 13.2 us -> 0.01 us
  other arithmetic: 8.58 us -> 0 us
  local copies, waits for them, and re-layouts: 1.14 us -> 6.34 us
    pallas_call x0 -> x1, Pallas kernels: none -> 118 us  [local(): pl.pallas_call(functools.partial(moe_kernel, cfg), out_shape=jax.ShapeDty...]
    reduce_scatter x2 -> x0, waiting for transfers between devices: 63.4 us -> none  [run_expert(): lax.psum_scatter(down_term.astype(jnp.bfloat16), 'tp', scatter_dimension=...]
    all_gather x2 -> x0, waiting for transfers between devices: 49.1 us -> none  [handle(): gathered = lax.all_gather(received, 'tp', axis=2, tiled=True)]
    all_to_all x2 -> x0, blocking collectives: 43.1 us -> none  [exchange_in_groups(): lax.all_to_all(group, axis, split_axis=split_dim, concat_axis=concat_dim,...]
    dot_general x6 -> x0, matrix products: 41.6 us -> none  [the longest x2 25.5 us: run_expert(): jnp.einsum('rf,fc->rc', hidden, w_down[0], preferred_element_type=jnp.flo...]
    all_to_all x3 -> x0, starting transfers between devices: 21 us -> none  [the longest x2 15.2 us: run_expert(): return lax.all_to_all(shares, 'ep', split_axis=0, concat_axis=0, tiled=True)]
    all_to_all x3 -> x0, waiting for transfers between devices: 13.8 us -> none  [the longest x2 13.8 us: run_expert(): return lax.all_to_all(shares, 'ep', split_axis=0, concat_axis=0, tiled=True)]
    unnamed x2 -> x3, local copies, waits for them, and re-layouts: 0.01 us -> 5.06 us
  transfers between devices with their start and end apart: 7 -> 0, of which waited for: 5 -> 0; matrix products, arithmetic and copies ran while one was open for 18% -> 0% of each run, Pallas kernels for 0% -> 0%
where the time goes in v1:
time: 124 us
  Pallas kernels  118 us (95%)
  local copies, waits for them, and re-layouts  6.34 us (5%)
    pallas_call x1, Pallas kernels, local(): pl.pallas_call(functools.partial(moe_kernel, cfg), out_shape=jax.ShapeDty...  118 us
    unnamed x3, local copies, waits for them, and re-layouts  5.06 us

profile of v1, /device:TPU:1, one launch (start us, length us, event | category | flops | bytes accessed | tf_op | source)
XLA Modules:
  0.0 124.2 jit_solution(9948314134531452876)
XLA Ops:
  0.0 1.3 %reshape.3.gain_ref = bf16[1,1792]{1,0:T(2,128)(2,1)} reshape(bf16[1792]{0:T(1024)(128)(2,1)} %param.8) | data formatting | bytes 7168 | tf_op jit(solution)/shard_map/reshape | solution.py:488
  1.3 1.4 %copy.9.prob_ref = bf16[256,8]{1,0:T(8,128)(2,1)} copy(bf16[256,8]{0,1:T(8,128)(2,1)} %param.10) | data formatting | bytes 8192 | tf_op args[3]
  2.7 1.5 %copy.8.ids_ref = s32[256,8]{1,0:T(8,128)} copy(s32[256,8]{0,1:T(8,128)} %param.9) | data formatting | bytes 16384 | tf_op args[2]
  4.2 117.8 %moe_layer.1 = bf16[256,1792]{1,0:T(8,128)(2,1)} custom-call(bf16[256,1792]{1,0:T(8,128)(2,1)} %tokens_ref.1, bf16[1,1792]{1,0:T(2,128)(2,1)} %reshape.3.gain_ref, s32[256,8]{1,0:T(8,128)} %copy.8.ids_ref, bf16[256,8]{1,0:T(8,128)(2,1)} %copy.9.prob_ref, bf16[7168,512]{1,0:T(8,128)(2,1)} %bitcast.3, bf16[7168,512]{1,0:T(8,128)(2,1)} %bitcast.4, ...), custom_call_target="tpu_custom_call" | custom-call | tf_op jit(solution)/shard_map/moe_layer/pallas_call | solution.py:478
  122.0 2.2 %copy.11 = bf16[256,1792]{1,0:T(8,128)(2,1)} copy(bf16[256,1792]{1,0:T(8,128)(2,1)} %moe_layer.1) | data formatting | bytes 1835008

commit v2 on v0

v2 whole, which is shorter than its diff:
```python
import functools

import jax
import jax.numpy as jnp
from jax import lax
from jax.experimental import pallas as pl
from jax.experimental.pallas import tpu as pltpu
from jax.sharding import PartitionSpec as P

MESH = pl.DeviceIdType.MESH
F32 = jnp.float32
BF16 = jnp.bfloat16

D = 7168
CAP = 16
CORES = 2
NZ = 4
WIDTHS_A = (256, 256, 256, 256)
WIDTHS_B = (256, 256, 256)
WEIGHT_PIECES = 4
epsilon = 1e-06


def moe_kernel(
    cfg,
    tokens_hbm,
    gain_ref,
    ids_ref,
    prob_ref,
    wg_hbm,
    wu_hbm,
    wd_hbm,
    out_ref,
    tokens,
    sc_out,
    sc_in,
    scales,
    wg,
    wu,
    wd,
    sq_buf,
    disp_t,
    comb,
    acc_g,
    acc_u,
    hid,
    t_sem,
    w_sem,
    sc_send,
    sc_recv,
    sq_send,
    sq_recv,
    per_a,
    per_b,
    sem_a,
    sem_b,
):
    xa, out_a, far_a, far_in_a, near_a, near_in_a, ret_a = per_a
    xb, nb, out_b, ret_b, far_b, far_in_b, near_b, near_in_b = per_b
    da_send, da_recv, za_send, za_recv, ra_send, ra_recv, ya_send, ya_recv = sem_a
    db_send, db_recv, zb_send, zb_recv, rb_send, rb_recv, yb_send, yb_recv = sem_b
    E, A, B = cfg["E"], cfg["A"], cfg["B"]
    NA, NB = len(A), len(B)
    DZ, T = cfg["DZ"], cfg["T"]
    S = E * CAP
    EH = E // 2
    SH = S // 2
    TH = T // 2
    e = lax.axis_index("ep")
    z = lax.axis_index("tp")
    zp = lax.rem(z + 1, NZ)
    zm = lax.rem(z + 3, NZ)
    zf = lax.rem(z + 2, NZ)

    def peer_of(k):
        off = lax.rem(k * cfg["STRIDE"], E)
        chip = lax.rem(e // CORES + off // CORES, E // CORES)
        if cfg["NX"] > 1:
            nx = cfg["NX"]
            oc = off // CORES
            mc = e // CORES
            py = lax.rem(mc // nx + oc // nx, E // CORES // nx)
            px = lax.rem(lax.rem(mc, nx) + lax.rem(oc, nx), nx)
            chip = py * nx + px
        core = lax.rem(lax.rem(e, CORES) + lax.rem(off, CORES), CORES)
        return chip * CORES + core

    def to_z(src, dst, send, recv, zt):
        return pltpu.make_async_remote_copy(
            src_ref=src, dst_ref=dst, send_sem=send, recv_sem=recv, device_id=(e, zt), device_id_type=MESH
        )

    def to_e(src, dst, send, recv, et):
        return pltpu.make_async_remote_copy(
            src_ref=src, dst_ref=dst, send_sem=send, recv_sem=recv, device_id=(et, z), device_id_type=MESH
        )

    def take(ref, sem):
        pltpu.make_async_copy(ref, ref, sem).wait()

    barrier = pltpu.get_barrier_semaphore()

    def greet(k, carry):
        pl.semaphore_signal(barrier, inc=1, device_id=(peer_of(k), z), device_id_type=MESH)
        return carry

    for dz in range(1, NZ):
        pl.semaphore_signal(barrier, inc=1, device_id=(e, lax.rem(z + dz, NZ)), device_id_type=MESH)
    lax.fori_loop(1, E, greet, 0)

    token_copy = pltpu.make_async_copy(tokens_hbm, tokens, t_sem)
    token_copy.start()
    rows_w = wg.shape[0] // WEIGHT_PIECES
    rows_d = wd.shape[0] // WEIGHT_PIECES
    weight_copies = []
    for p in range(WEIGHT_PIECES):
        rs = pl.ds(p * rows_w, rows_w)
        weight_copies.append(pltpu.make_async_copy(wg_hbm.at[rs], wg.at[rs], w_sem.at[0, p]))
        weight_copies.append(pltpu.make_async_copy(wu_hbm.at[rs], wu.at[rs], w_sem.at[1, p]))
    down_copies = []
    for p in range(WEIGHT_PIECES):
        rs = pl.ds(p * rows_d, rows_d)
        down_copies.append(pltpu.make_async_copy(wd_hbm.at[rs], wd.at[rs], w_sem.at[2, p]))

    ids = ids_ref[...]
    probs = prob_ref[...].astype(F32)
    expert_iota = lax.broadcasted_iota(jnp.int32, (E, T), 0)
    match = jnp.zeros((E, T), F32)
    weight = jnp.zeros((E, T), F32)
    for k in range(ids.shape[0]):
        hit = ids[k : k + 1, :] == expert_iota
        match = match + jnp.where(hit, 1.0, 0.0)
        weight = weight + jnp.where(hit, probs[k : k + 1, :], 0.0)
    earlier = jnp.where(
        lax.broadcasted_iota(jnp.int32, (T, T), 0) < lax.broadcasted_iota(jnp.int32, (T, T), 1), 1.0, 0.0
    ).astype(BF16)
    match_b = match.astype(BF16)
    before = jnp.dot(match_b, earlier, preferred_element_type=F32).astype(BF16)
    spread = jnp.where(
        lax.broadcasted_iota(jnp.int32, (S, E), 0) // CAP == lax.broadcasted_iota(jnp.int32, (S, E), 1), 1.0, 0.0
    )
    spread_b = spread.astype(BF16)
    match_s = jnp.dot(spread_b, match_b, preferred_element_type=F32)
    before_s = jnp.dot(spread_b, before, preferred_element_type=F32)
    weight_s = jnp.dot(spread_b, weight.astype(BF16), preferred_element_type=F32)
    slot_of = lax.rem(lax.broadcasted_iota(jnp.int32, (S, T), 0), CAP).astype(F32)
    chosen = jnp.where((match_s > 0.5) & (before_s == slot_of), 1.0, 0.0)
    disp_t[...] = chosen.astype(BF16)
    token_copy.wait()
    for copy in weight_copies + down_copies:
        copy.start()

    def scaled(at):
        lo, w = at
        gain = gain_ref[pl.ds(lo, w)].astype(F32).reshape(1, w)
        return (tokens[:, pl.ds(lo, w)].astype(F32) * gain).astype(BF16)

    def to_all(src, dst, send, recv):
        def one(k, carry):
            et = peer_of(k)
            to_e(src.at[et], dst, send, recv, et).start()
            return carry

        lax.fori_loop(1, E, one, 0)

    def scale_b(c):
        nb[c][z] = scaled(B[c])

    def direct_b(c):
        for i, zt in ((0, zp), (1, zm)):
            to_z(nb[c].at[z], nb[c].at[z], zb_send.at[i, c], zb_recv.at[i, c], zt).start()

    def dispatch_a(c):
        rows = jnp.dot(disp_t[...], scaled(A[c]), preferred_element_type=F32).astype(BF16)
        out_a[c][...] = rows.reshape(E, CAP, A[c][1])
        to_all(out_a[c], xa[c].at[z, e], da_send.at[c], da_recv.at[c])
        xa[c][z, e] = out_a[c][e]

    def squares():
        TP = max(T, 128)
        values = tokens[...].astype(F32)
        part = jnp.sum(values * values, axis=1, keepdims=True)
        if T < 128:
            part = jnp.concatenate([part, jnp.zeros((128 - T, 1), F32)], axis=0)
        part_t = jnp.transpose(jnp.broadcast_to(part, (TP, 128)))
        sq_buf[z] = part_t[0:8, :]
        for copy in sq_copies:
            copy.start()

    sq_copies = [
        to_z(sq_buf.at[z], sq_buf.at[z], sq_send.at[dz - 1], sq_recv.at[dz - 1], lax.rem(z + dz, NZ))
        for dz in range(1, NZ)
    ]

    def prepare():
        comb[...] = jnp.transpose(chosen * weight_s).astype(BF16)
        acc_g[...] = jnp.zeros_like(acc_g)
        acc_u[...] = jnp.zeros_like(acc_u)

    def lane_of_slot():
        lane = lax.broadcasted_iota(jnp.int32, (S, 128), 1)
        return lane == lax.rem(lax.broadcasted_iota(jnp.int32, (S, 128), 0), CAP)

    def send_scales():
        for copy in sq_copies:
            copy.wait()
        total = (sq_buf[0] + sq_buf[1] + sq_buf[2] + sq_buf[3])[0:1, 0:T]
        inverse = lax.rsqrt(total / cfg["D"] + epsilon)
        per_slot = jnp.sum(disp_t[...].astype(F32) * inverse, axis=1, keepdims=True)
        laned = jnp.where(lane_of_slot(), per_slot, 0.0)
        owner = jnp.where(
            lax.broadcasted_iota(jnp.int32, (E, S), 1) // CAP == lax.broadcasted_iota(jnp.int32, (E, S), 0), 1.0, 0.0
        )
        table = jnp.dot(owner, laned, preferred_element_type=F32, precision=lax.Precision.HIGHEST)
        sc_out[...] = table.reshape(E, 1, 128)
        to_all(sc_out, sc_in.at[e], sc_send.at[0], sc_recv.at[0])
        sc_in[e] = sc_out[e]

    def take_scales():
        take(sc_in.at[pl.ds(0, E - 1)], sc_recv.at[0])
        owner = jnp.where(
            lax.broadcasted_iota(jnp.int32, (S, E), 0) // CAP == lax.broadcasted_iota(jnp.int32, (S, E), 1), 1.0, 0.0
        )
        rows = jnp.dot(
            owner, sc_in[...].reshape(E, 128), preferred_element_type=F32, precision=lax.Precision.HIGHEST
        )
        per_row = jnp.sum(jnp.where(lane_of_slot(), rows, 0.0), axis=1, keepdims=True)
        scales[...] = jnp.broadcast_to(per_row, (S, 128))

    def forward_b(c):
        lo, hi = pl.ds(0, TH), pl.ds(TH, TH)
        take(nb[c].at[zm], zb_recv.at[0, c])
        to_z(nb[c].at[zm, lo], nb[c].at[zm, lo], zb_send.at[2, c], zb_recv.at[2, c], zp).start()
        take(nb[c].at[zp], zb_recv.at[1, c])
        to_z(nb[c].at[zp, hi], nb[c].at[zp, hi], zb_send.at[3, c], zb_recv.at[3, c], zm).start()

    def dispatch_b(c):
        take(nb[c].at[zf, pl.ds(0, TH)], zb_recv.at[2, c])
        take(nb[c].at[zf, pl.ds(TH, TH)], zb_recv.at[3, c])
        for q in range(NZ):
            rows = jnp.dot(disp_t[...], nb[c][q], preferred_element_type=F32).astype(BF16)
            out_b[c][:, q] = rows.reshape(E, CAP, B[c][1])
        to_all(out_b[c], xb[c].at[e], db_send.at[c], db_recv.at[c])
        xb[c][e] = out_b[c][e]

    def direct_a(c):
        take(xa[c].at[z, pl.ds(0, E - 1)], da_recv.at[c])
        for i, zt in ((0, zp), (1, zm)):
            to_z(xa[c].at[z], xa[c].at[z], za_send.at[i, c], za_recv.at[i, c], zt).start()

    def forward_a(c):
        lo, hi = pl.ds(0, EH), pl.ds(EH, EH)
        take(xa[c].at[zm], za_recv.at[0, c])
        to_z(xa[c].at[zm, lo], xa[c].at[zm, lo], za_send.at[2, c], za_recv.at[2, c], zp).start()
        take(xa[c].at[zp], za_recv.at[1, c])
        to_z(xa[c].at[zp, hi], xa[c].at[zp, hi], za_send.at[3, c], za_recv.at[3, c], zm).start()

    def multiply(blocks, at):
        base, width = at
        x = jnp.concatenate([b.reshape(S, width) for b, _ in blocks], axis=1)
        for w_ref, acc in ((wg, acc_g), (wu, acc_u)):
            w = jnp.concatenate(
                [w_ref[pl.ds(pl.multiple_of(q * DZ + base, 128), width), :] for _, q in blocks], axis=0
            )
            acc[...] += jnp.dot(x, w, preferred_element_type=F32)

    def multiply_near(c):
        multiply([(xa[c][q], q) for q in (z, zp, zm)], A[c])

    def multiply_far(c):
        take(xa[c].at[zf, pl.ds(0, EH)], za_recv.at[2, c])
        take(xa[c].at[zf, pl.ds(EH, EH)], za_recv.at[3, c])
        multiply([(xa[c][zf], zf)], A[c])

    def multiply_b(c):
        take(xb[c].at[pl.ds(0, E - 1)], db_recv.at[c])
        multiply([(xb[c][:, q], q) for q in range(NZ)], B[c])

    def wait_weights():
        for copy in weight_copies:
            copy.wait()

    def enter():
        pl.semaphore_wait(barrier, E - 1 + NZ - 1)

    def run(plan):
        for name, *index in plan:
            with jax.named_scope(name):
                steps[name](*index)

    steps = dict(
        (fn.__name__, fn)
        for fn in (
            enter, scale_b, direct_b, dispatch_a, squares, prepare, send_scales, take_scales, forward_b,
            dispatch_b, direct_a, forward_a, multiply_near, multiply_far, multiply_b, wait_weights,
        )
    )
    run(cfg["OUT_PLAN"])

    s = scales[:, 0:1]
    g = acc_g[...] * s
    hid[...] = (g / (1.0 + jnp.exp(-g)) * (acc_u[...] * s)).astype(BF16)
    for copy in down_copies:
        copy.wait()

    def down(q, at):
        lo, w = at
        ds = pl.ds(pl.multiple_of(q * DZ + lo, 128), w)
        return jnp.dot(hid[...], wd[:, ds], preferred_element_type=F32).astype(BF16)

    lo_s, hi_s = pl.ds(0, SH), pl.ds(SH, SH)
    lo_t, hi_t = pl.ds(0, TH), pl.ds(TH, TH)

    def plus(a, b):
        return (a.astype(F32) + b.astype(F32)).astype(BF16)

    def far_part_a(c):
        far_a[c][...] = down(zf, A[c])
        to_z(far_a[c].at[lo_s], far_in_a[c].at[lo_s], ra_send.at[0, c], ra_recv.at[0, c], zp).start()
        to_z(far_a[c].at[hi_s], far_in_a[c].at[hi_s], ra_send.at[1, c], ra_recv.at[1, c], zm).start()

    def near_part_a(c):
        near_a[c][0] = down(zp, A[c])
        near_a[c][1] = down(zm, A[c])
        take(far_in_a[c].at[lo_s], ra_recv.at[0, c])
        near_a[c][0, lo_s] = plus(near_a[c][0, lo_s], far_in_a[c][lo_s])
        to_z(near_a[c].at[0], near_in_a[c].at[0], ra_send.at[2, c], ra_recv.at[2, c], zp).start()
        take(far_in_a[c].at[hi_s], ra_recv.at[1, c])
        near_a[c][1, hi_s] = plus(near_a[c][1, hi_s], far_in_a[c][hi_s])
        to_z(near_a[c].at[1], near_in_a[c].at[1], ra_send.at[3, c], ra_recv.at[3, c], zm).start()

    def own_part_a(c):
        own = down(z, A[c]).astype(F32)
        take(near_in_a[c].at[0], ra_recv.at[2, c])
        take(near_in_a[c].at[1], ra_recv.at[3, c])
        own = own + near_in_a[c][0].astype(F32) + near_in_a[c][1].astype(F32)
        out_a[c][...] = own.astype(BF16).reshape(E, CAP, A[c][1])
        to_all(out_a[c], ret_a[c].at[e], ya_send.at[c], ya_recv.at[c])
        ret_a[c][e] = out_a[c][e]

    def part_b(c):
        for q in range(NZ):
            out_b[c][:, q] = down(q, B[c]).reshape(E, CAP, B[c][1])
        to_all(out_b[c], ret_b[c].at[e], yb_send.at[c], yb_recv.at[c])
        ret_b[c][e] = out_b[c][e]

    def weigh_b(c, q):
        return jnp.dot(comb[...], ret_b[c][:, q].reshape(S, B[c][1]), preferred_element_type=F32)

    def far_part_b(c):
        take(ret_b[c].at[pl.ds(0, E - 1)], yb_recv.at[c])
        far_b[c][...] = weigh_b(c, zf).astype(BF16)
        to_z(far_b[c].at[lo_t], far_in_b[c].at[lo_t], rb_send.at[0, c], rb_recv.at[0, c], zp).start()
        to_z(far_b[c].at[hi_t], far_in_b[c].at[hi_t], rb_send.at[1, c], rb_recv.at[1, c], zm).start()

    def near_part_b(c):
        near_b[c][0] = weigh_b(c, zp).astype(BF16)
        near_b[c][1] = weigh_b(c, zm).astype(BF16)
        take(far_in_b[c].at[lo_t], rb_recv.at[0, c])
        near_b[c][0, lo_t] = plus(near_b[c][0, lo_t], far_in_b[c][lo_t])
        to_z(near_b[c].at[0], near_in_b[c].at[0], rb_send.at[2, c], rb_recv.at[2, c], zp).start()
        take(far_in_b[c].at[hi_t], rb_recv.at[1, c])
        near_b[c][1, hi_t] = plus(near_b[c][1, hi_t], far_in_b[c][hi_t])
        to_z(near_b[c].at[1], near_in_b[c].at[1], rb_send.at[3, c], rb_recv.at[3, c], zm).start()

    def own_part_b(c):
        own = weigh_b(c, z)
        take(near_in_b[c].at[0], rb_recv.at[2, c])
        take(near_in_b[c].at[1], rb_recv.at[3, c])
        own = own + near_in_b[c][0].astype(F32) + near_in_b[c][1].astype(F32)
        out_ref[:, pl.ds(*B[c])] = own.astype(BF16)

    def combine_a(c):
        take(ret_a[c].at[pl.ds(0, E - 1)], ya_recv.at[c])
        got = jnp.dot(comb[...], ret_a[c][...].reshape(S, A[c][1]), preferred_element_type=F32)
        out_ref[:, pl.ds(*A[c])] = got.astype(BF16)

    rest = pl.ds(0, E - 1)
    for c in range(NA):
        take(out_a[c].at[rest], da_send.at[c])
    for c in range(NB):
        take(out_b[c].at[rest], db_send.at[c])
    take(sc_out.at[rest], sc_send.at[0])

    steps.update(
        (fn.__name__, fn)
        for fn in (far_part_a, near_part_a, own_part_a, part_b, far_part_b, near_part_b, own_part_b, combine_a)
    )
    run(cfg["BACK_PLAN"])

    for c in range(NA):
        for i in range(2):
            take(xa[c].at[0], za_send.at[i, c])
            take(xa[c].at[0, pl.ds(0, EH)], za_send.at[2 + i, c])
            take(far_a[c].at[lo_s], ra_send.at[i, c])
            take(near_a[c].at[0], ra_send.at[2 + i, c])
        take(out_a[c].at[rest], ya_send.at[c])
    for c in range(NB):
        for i in range(2):
            take(nb[c].at[0], zb_send.at[i, c])
            take(nb[c].at[0, pl.ds(0, TH)], zb_send.at[2 + i, c])
            take(far_b[c].at[lo_t], rb_send.at[i, c])
            take(near_b[c].at[0], rb_send.at[2 + i, c])
        take(out_b[c].at[rest], yb_send.at[c])


OUT_PLAN = (
    "scale_b 0",
    "scale_b 1",
    "enter",
    "direct_b 0",
    "direct_b 1",
    "dispatch_a 0",
    "dispatch_a 1",
    "dispatch_a 2",
    "squares",
    "scale_b 2",
    "forward_b 0",
    "direct_b 2",
    "dispatch_a 3",
    "dispatch_a 4",
    "prepare",
    "forward_b 1",
    "dispatch_b 0",
    "direct_a 0",
    "forward_b 2",
    "send_scales",
    "dispatch_b 1",
    "direct_a 1",
    "dispatch_b 2",
    "wait_weights",
    "forward_a 0",
    "direct_a 2",
    "multiply_near 0",
    "forward_a 1",
    "direct_a 3",
    "multiply_near 1",
    "multiply_far 0",
    "take_scales",
    "multiply_b 0",
    "forward_a 2",
    "direct_a 4",
    "multiply_near 2",
    "multiply_far 1",
    "multiply_b 1",
    "forward_a 3",
    "multiply_near 3",
    "multiply_far 2",
    "forward_a 4",
    "multiply_near 4",
    "multiply_b 2",
    "multiply_far 3",
    "multiply_far 4",
)
BACK_PLAN = (
    "far_part_a 0",
    "part_b 0",
    "far_part_a 1",
    "part_b 1",
    "near_part_a 0",
    "far_part_a 2",
    "part_b 2",
    "near_part_a 1",
    "own_part_a 0",
    "far_part_b 0",
    "far_part_a 3",
    "near_part_a 2",
    "near_part_b 0",
    "own_part_a 1",
    "far_part_a 4",
    "near_part_a 3",
    "own_part_a 2",
    "far_part_b 1",
    "near_part_a 4",
    "near_part_b 1",
    "own_part_a 3",
    "far_part_b 2",
    "own_part_a 4",
    "near_part_b 2",
    "combine_a 0",
    "combine_a 1",
    "combine_a 2",
    "own_part_b 0",
    "own_part_b 1",
    "combine_a 3",
    "combine_a 4",
    "own_part_b 2",
)


def steps_of(text, na, nb):
    plan = []
    for step in text:
        name, *index = step.split(" ")
        index = [int(i) for i in index]
        if index and index[0] >= (nb if name.endswith("_b") else na):
            continue
        plan.append((name, *index))
    return plan


def local(cfg, tokens, norm_gain, expert_ids, gate_prob, w_gate, w_up, w_down):
    E, T, A, B = cfg["E"], cfg["T"], cfg["A"], cfg["B"]
    DZ, FFD = cfg["DZ"], cfg["FFD"]
    S = E * CAP
    vmem = pl.BlockSpec(memory_space=pltpu.VMEM)
    hbm = pl.BlockSpec(memory_space=pl.ANY)
    TP = max(T, 128)
    dma = pltpu.SemaphoreType.DMA

    def each(chunks, *shape):
        return [pltpu.VMEM((*shape, w), BF16) for _, w in chunks]

    def sems(n):
        return [dma((n,)), dma((n,)), dma((4, n)), dma((4, n)), dma((4, n)), dma((4, n)), dma((n,)), dma((n,))]

    scratch = [
        pltpu.VMEM((T, DZ), BF16),
        pltpu.VMEM((E, 1, 128), F32),
        pltpu.VMEM((E, 1, 128), F32),
        pltpu.VMEM((S, 128), F32),
        pltpu.VMEM((NZ * DZ, FFD), BF16),
        pltpu.VMEM((NZ * DZ, FFD), BF16),
        pltpu.VMEM((FFD, NZ * DZ), BF16),
        pltpu.VMEM((NZ, 8, TP), F32),
        pltpu.VMEM((S, T), BF16),
        pltpu.VMEM((T, S), BF16),
        pltpu.VMEM((S, FFD), F32),
        pltpu.VMEM((S, FFD), F32),
        pltpu.VMEM((S, FFD), BF16),
        dma,
        dma((3, WEIGHT_PIECES)),
        dma((1,)),
        dma((1,)),
        dma((NZ - 1,)),
        dma((NZ - 1,)),
        [
            each(A, NZ, E, CAP),
            each(A, E, CAP),
            each(A, S),
            each(A, S),
            each(A, 2, S),
            each(A, 2, S),
            each(A, E, CAP),
        ],
        [
            each(B, E, NZ, CAP),
            each(B, NZ, T),
            each(B, E, NZ, CAP),
            each(B, E, NZ, CAP),
            each(B, T),
            each(B, T),
            each(B, 2, T),
            each(B, 2, T),
        ],
        sems(len(A)),
        sems(len(B)),
    ]
    return pl.pallas_call(
        functools.partial(moe_kernel, cfg),
        out_shape=jax.ShapeDtypeStruct((T, DZ), BF16),
        in_specs=[hbm, vmem, vmem, vmem, hbm, hbm, hbm],
        out_specs=vmem,
        scratch_shapes=scratch,
        compiler_params=pltpu.CompilerParams(
            collective_id=0, has_side_effects=True, vmem_limit_bytes=cfg["VMEM"]
        ),
        name="moe_layer",
    )(tokens, norm_gain, expert_ids.T, gate_prob.T, w_gate[0], w_up[0], w_down[0])


def config(mesh, tokens=8192, width=D, ff=2048, a=WIDTHS_A, b=WIDTHS_B, nx=4):
    E = mesh.shape["ep"]
    DZ = width // NZ
    chunks, lo = [], 0
    for w in (*a, *b):
        chunks.append((lo, w))
        lo += w
    assert lo == DZ
    return dict(
        E=E,
        T=tokens // E,
        D=width,
        DZ=DZ,
        FFD=ff // NZ,
        A=chunks[: len(a)],
        B=chunks[len(a) :],
        NX=nx,
        STRIDE=11,
        VMEM=67_000_000,
        OUT_PLAN=steps_of(OUT_PLAN, len(a), len(b)),
        BACK_PLAN=steps_of(BACK_PLAN, len(a), len(b)),
    )


def build(mesh, cfg):
    placed = (
        P("ep", "tp"),
        P("tp"),
        P("ep", None),
        P("ep", None),
        P("ep", None, "tp"),
        P("ep", None, "tp"),
        P("ep", "tp", None),
    )
    return jax.shard_map(
        functools.partial(local, cfg), mesh=mesh, in_specs=placed, out_specs=P("ep", "tp"), check_vma=False
    )


def solution(mesh):
    return build(mesh, config(mesh))
```

time: 256 us -> 116 us (0.45)
  waiting for transfers between devices: 126 us -> 0 us
  Pallas kernels: 0 us -> 114 us
  blocking collectives: 43.1 us -> 0 us
  matrix products: 41.6 us -> 0 us
  starting transfers between devices: 21.3 us -> 0 us
  between operations: 13.2 us -> 0.01 us
  other arithmetic: 8.58 us -> 0 us
    pallas_call x0 -> x1, Pallas kernels: none -> 114 us  [local(): pl.pallas_call(functools.partial(moe_kernel, cfg), out_shape=jax.ShapeDty...]
    reduce_scatter x2 -> x0, waiting for transfers between devices: 63.4 us -> none  [run_expert(): lax.psum_scatter(down_term.astype(jnp.bfloat16), 'tp', scatter_dimension=...]
    all_gather x2 -> x0, waiting for transfers between devices: 49.1 us -> none  [handle(): gathered = lax.all_gather(received, 'tp', axis=2, tiled=True)]
    all_to_all x2 -> x0, blocking collectives: 43.1 us -> none  [exchange_in_groups(): lax.all_to_all(group, axis, split_axis=split_dim, concat_axis=concat_dim,...]
    dot_general x6 -> x0, matrix products: 41.6 us -> none  [the longest x2 25.5 us: run_expert(): jnp.einsum('rf,fc->rc', hidden, w_down[0], preferred_element_type=jnp.flo...]
    all_to_all x3 -> x0, starting transfers between devices: 21 us -> none  [the longest x2 15.2 us: run_expert(): return lax.all_to_all(shares, 'ep', split_axis=0, concat_axis=0, tiled=True)]
    all_to_all x3 -> x0, waiting for transfers between devices: 13.8 us -> none  [the longest x2 13.8 us: run_expert(): return lax.all_to_all(shares, 'ep', split_axis=0, concat_axis=0, tiled=True)]
    reduce_sum x5 -> x0, other arithmetic: 4.64 us -> none  [the longest x1 1.69 us: place_picks(): jnp.sum(jnp.where(hit_table, gate_prob.astype(jnp.float32)[:, :, None], 0...]
  transfers between devices with their start and end apart: 7 -> 0, of which waited for: 5 -> 0; matrix products, arithmetic and copies ran while one was open for 18% -> 0% of each run, Pallas kernels for 0% -> 0%
where the time goes in v2:
time: 116 us
  Pallas kernels  114 us (98%)
  local copies, waits for them, and re-layouts  2.16 us (2%)
    pallas_call x1, Pallas kernels, local(): pl.pallas_call(functools.partial(moe_kernel, cfg), out_shape=jax.ShapeDty...  114 us

profile of v2, /device:TPU:1, one launch (start us, length us, event | category | flops | bytes accessed | tf_op | source)
XLA Modules:
  0.0 115.8 jit_solution(2635453232063641688)
XLA Ops:
  0.0 113.6 %moe_layer.1 = bf16[256,1792]{1,0:T(8,128)(2,1)} custom-call(bf16[256,1792]{1,0:T(8,128)(2,1)} %tokens_hbm.1, bf16[1792]{0:T(1024)(128)(2,1)} %gain_ref.1, s32[8,256]{1,0:T(8,128)} %bitcast.8, bf16[8,256]{1,0:T(8,128)(2,1)} %bitcast.9, bf16[7168,512]{1,0:T(8,128)(2,1)} %bitcast.5, bf16[7168,512]{1,0:T(8,128)(2,1)} %bitcast.6, bf16[512,7168]{1,0:T(8,128)(2,1)} %bitcast.7), custom_call_target="tpu_custom_call" | custom-call | tf_op jit(solution)/shard_map/moe_layer/pallas_call | solution.py:559
  113.6 2.2 %copy.9 = bf16[256,1792]{1,0:T(8,128)(2,1)} copy(bf16[256,1792]{1,0:T(8,128)(2,1)} %moe_layer.1) | data formatting | bytes 1835008

commit v3 on v2

v3 whole, which is shorter than its diff:
```python
import functools

import jax
import jax.numpy as jnp
from jax import lax
from jax.experimental import pallas as pl
from jax.experimental.pallas import tpu as pltpu
from jax.sharding import PartitionSpec as P

MESH = pl.DeviceIdType.MESH
F32 = jnp.float32
BF16 = jnp.bfloat16

D = 7168
CAP = 16
CORES = 2
NZ = 4
WIDTHS_A = (256, 256, 256, 256)
WIDTHS_B = (256, 256, 256)
WEIGHT_PIECES = 4
epsilon = 1e-06


def moe_kernel(
    cfg,
    tokens_hbm,
    gain_hbm,
    ids_hbm,
    prob_hbm,
    wg_hbm,
    wu_hbm,
    wd_hbm,
    out_hbm,
    tokens,
    gain_ref,
    ids_ref,
    prob_ref,
    out_v,
    sc_out,
    sc_in,
    scales,
    wg,
    wu,
    wd,
    sq_buf,
    disp_t,
    comb,
    acc_g,
    acc_u,
    hid,
    t_sem,
    o_sem,
    w_sem,
    sent,
    sc_recv,
    sq_recv,
    per_a,
    per_b,
    sem_a,
    sem_b,
):
    xa, out_a, far_a, far_in_a, near_a, near_in_a, back_a, ret_a = per_a
    xb, nb, out_b, back_b, ret_b, far_b, far_in_b, near_b, near_in_b = per_b
    da_recv, za_recv, ra_recv, ya_recv = sem_a
    db_recv, zb_recv, rb_recv, yb_recv = sem_b
    da_send, db_send, za_send, zb_send, ra_send, rb_send, ya_send, yb_send, sc_send, sq_send = (
        sent.at[i] for i in range(10)
    )
    E, A, B = cfg["E"], cfg["A"], cfg["B"]
    NA, NB = len(A), len(B)
    DZ, T = cfg["DZ"], cfg["T"]
    S = E * CAP
    EH, EQ = E // 2, E // 4
    SH, SQ = S // 2, S // 4
    TH = T // 2
    e = lax.axis_index("ep")
    z = lax.axis_index("tp")
    zp = lax.rem(z + 1, NZ)
    zm = lax.rem(z + 3, NZ)
    zf = lax.rem(z + 2, NZ)

    def moved(off, sign):
        off = jnp.int32(off)
        nx, ny = cfg["NX"], E // CORES // cfg["NX"]
        mine, step = e // CORES, off // CORES
        py = lax.rem(mine // nx + sign * (step // nx) + ny, ny)
        px = lax.rem(lax.rem(mine, nx) + sign * lax.rem(step, nx) + nx, nx)
        core = lax.rem(lax.rem(e, CORES) + sign * lax.rem(off, CORES) + CORES, CORES)
        return (py * nx + px) * CORES + core

    def peer_of(k):
        return moved(lax.rem(k * cfg["STRIDE"], E), 1)

    def origin_of(k):
        return moved(lax.rem(k * cfg["STRIDE"], E), -1)

    def to_z(src, dst, send, recv, zt):
        return pltpu.make_async_remote_copy(
            src_ref=src, dst_ref=dst, send_sem=send, recv_sem=recv, device_id=(e, zt), device_id_type=MESH
        )

    def to_e(src, dst, send, recv, et):
        return pltpu.make_async_remote_copy(
            src_ref=src, dst_ref=dst, send_sem=send, recv_sem=recv, device_id=(et, z), device_id_type=MESH
        )

    def take(ref, sem):
        pltpu.make_async_copy(ref, ref, sem).wait()

    small_copies = [
        pltpu.make_async_copy(src, dst, t_sem.at[n])
        for n, (src, dst) in enumerate(
            ((ids_hbm, ids_ref), (prob_hbm, prob_ref), (gain_hbm, gain_ref), (tokens_hbm, tokens))
        )
    ]
    for copy in small_copies:
        copy.start()
    barrier = pltpu.get_barrier_semaphore()

    def hops(k):
        step, nx, ny = k // CORES, cfg["NX"], E // CORES // cfg["NX"]
        dx, dy = step % nx, step // nx
        return min(dx, nx - dx) + min(dy, ny - dy)

    for k in sorted(range(1, E), key=hops, reverse=True):
        pl.semaphore_signal(barrier, inc=1, device_id=(moved(k, 1), z), device_id_type=MESH)
    for dz in (2, 1, 3):
        pl.semaphore_signal(barrier, inc=1, device_id=(e, lax.rem(z + dz, NZ)), device_id_type=MESH)
    for copy in small_copies[:3]:
        copy.wait()

    rows_w = wg.shape[0] // WEIGHT_PIECES
    rows_d = wd.shape[0] // WEIGHT_PIECES
    weight_copies = []
    for p in range(WEIGHT_PIECES):
        rs = pl.ds(p * rows_w, rows_w)
        weight_copies.append(pltpu.make_async_copy(wg_hbm.at[rs], wg.at[rs], w_sem.at[0]))
        weight_copies.append(pltpu.make_async_copy(wu_hbm.at[rs], wu.at[rs], w_sem.at[1]))
    down_copies = []
    for p in range(WEIGHT_PIECES):
        rs = pl.ds(p * rows_d, rows_d)
        down_copies.append(pltpu.make_async_copy(wd_hbm.at[rs], wd.at[rs], w_sem.at[2]))

    ids = ids_ref[...]
    probs = prob_ref[...].astype(F32)
    expert_iota = lax.broadcasted_iota(jnp.int32, (E, T), 0)
    match = jnp.zeros((E, T), F32)
    weight = jnp.zeros((E, T), F32)
    for k in range(ids.shape[0]):
        hit = ids[k : k + 1, :] == expert_iota
        match = match + jnp.where(hit, 1.0, 0.0)
        weight = weight + jnp.where(hit, probs[k : k + 1, :], 0.0)
    earlier = jnp.where(
        lax.broadcasted_iota(jnp.int32, (T, T), 0) < lax.broadcasted_iota(jnp.int32, (T, T), 1), 1.0, 0.0
    ).astype(BF16)
    match_b = match.astype(BF16)
    before = jnp.dot(match_b, earlier, preferred_element_type=F32).astype(BF16)
    spread = jnp.where(
        lax.broadcasted_iota(jnp.int32, (S, E), 0) // CAP == lax.broadcasted_iota(jnp.int32, (S, E), 1), 1.0, 0.0
    )
    spread_b = spread.astype(BF16)
    match_s = jnp.dot(spread_b, match_b, preferred_element_type=F32)
    before_s = jnp.dot(spread_b, before, preferred_element_type=F32)
    weight_s = jnp.dot(spread_b, weight.astype(BF16), preferred_element_type=F32)
    slot_of = lax.rem(lax.broadcasted_iota(jnp.int32, (S, T), 0), CAP).astype(F32)
    chosen = jnp.where((match_s > 0.5) & (before_s == slot_of), 1.0, 0.0)
    disp_t[...] = chosen.astype(BF16)
    small_copies[3].wait()
    for copy in weight_copies + down_copies:
        copy.start()

    def scaled(at):
        lo, w = at
        gain = gain_ref[pl.ds(lo, w)].astype(F32).reshape(1, w)
        return (tokens[:, pl.ds(lo, w)].astype(F32) * gain).astype(BF16)

    def to_experts(src, dst, send, recv, h):
        def one(k, carry):
            et = peer_of(k)
            to_e(src.at[et], dst.at[k], send, recv, et).start()
            return carry

        lax.fori_loop(max(1, h * EH), (h + 1) * EH, one, 0)

    def to_origins(src, dst, send, recv, h):
        def one(k, carry):
            to_e(src.at[k], dst.at[e], send, recv, origin_of(k)).start()
            return carry

        lax.fori_loop(max(1, h * EH), (h + 1) * EH, one, 0)

    def half(h):
        return pl.ds(h * EH, EH)

    rest = pl.ds(0, E - 1)

    def others(h):
        return pl.ds(0, EH - 1 if h == 0 else EH)

    def scale_b(c):
        nb[c][z] = scaled(B[c])

    def direct_b(c):
        for i, zt in ((0, zp), (1, zm)):
            to_z(nb[c].at[z], nb[c].at[z], zb_send, zb_recv.at[0, c], zt).start()

    def dispatch_a(c, h):
        if h == 0:
            rows = jnp.dot(disp_t[...], scaled(A[c]), preferred_element_type=F32).astype(BF16)
            out_a[c][...] = rows.reshape(E, CAP, A[c][1])
        to_experts(out_a[c], xa[c].at[z], da_send, da_recv.at[c, h], h)
        if h == 0:
            xa[c][z, 0] = out_a[c][e]

    def squares():
        TP = max(T, 128)
        values = tokens[...].astype(F32)
        part = jnp.sum(values * values, axis=1, keepdims=True)
        if T < 128:
            part = jnp.concatenate([part, jnp.zeros((128 - T, 1), F32)], axis=0)
        part_t = jnp.transpose(jnp.broadcast_to(part, (TP, 128)))
        sq_buf[z] = part_t[0:8, :]
        for copy in sq_copies:
            copy.start()

    sq_copies = [
        to_z(sq_buf.at[z], sq_buf.at[z], sq_send, sq_recv.at[0], lax.rem(z + dz, NZ))
        for dz in range(1, NZ)
    ]

    def prepare():
        comb[...] = jnp.transpose(chosen * weight_s).astype(BF16)
        acc_g[...] = jnp.zeros_like(acc_g)
        acc_u[...] = jnp.zeros_like(acc_u)

    def lane_of_slot():
        lane = lax.broadcasted_iota(jnp.int32, (S, 128), 1)
        return lane == lax.rem(lax.broadcasted_iota(jnp.int32, (S, 128), 0), CAP)

    def send_scales():
        take(sq_buf.at[pl.ds(0, NZ - 1)], sq_recv.at[0])
        total = (sq_buf[0] + sq_buf[1] + sq_buf[2] + sq_buf[3])[0:1, 0:T]
        inverse = lax.rsqrt(total / cfg["D"] + epsilon)
        per_slot = jnp.sum(disp_t[...].astype(F32) * inverse, axis=1, keepdims=True)
        laned = jnp.where(lane_of_slot(), per_slot, 0.0)
        owner = jnp.where(
            lax.broadcasted_iota(jnp.int32, (E, S), 1) // CAP == lax.broadcasted_iota(jnp.int32, (E, S), 0), 1.0, 0.0
        )
        table = jnp.dot(owner, laned, preferred_element_type=F32, precision=lax.Precision.HIGHEST)
        sc_out[...] = table.reshape(E, 1, 128)
        for h in range(2):
            to_experts(sc_out, sc_in, sc_send, sc_recv.at[h], h)
        sc_in[0] = sc_out[e]

    def take_scales():
        for h in range(2):
            take(sc_in.at[others(h)], sc_recv.at[h])
        owner = jnp.where(
            lax.broadcasted_iota(jnp.int32, (S, E), 0) // CAP == lax.broadcasted_iota(jnp.int32, (S, E), 1), 1.0, 0.0
        )
        rows = jnp.dot(
            owner, sc_in[...].reshape(E, 128), preferred_element_type=F32, precision=lax.Precision.HIGHEST
        )
        per_row = jnp.sum(jnp.where(lane_of_slot(), rows, 0.0), axis=1, keepdims=True)
        scales[...] = jnp.broadcast_to(per_row, (S, 128))

    def forward_b(c):
        lo, hi = pl.ds(0, TH), pl.ds(TH, TH)
        take(nb[c].at[pl.ds(0, 2)], zb_recv.at[0, c])
        to_z(nb[c].at[zm, lo], nb[c].at[zm, lo], zb_send, zb_recv.at[1, c], zp).start()
        to_z(nb[c].at[zp, hi], nb[c].at[zp, hi], zb_send, zb_recv.at[1, c], zm).start()

    def dispatch_b(c, h):
        if h == 0:
            take(nb[c].at[zf], zb_recv.at[1, c])
            for q in range(NZ):
                rows = jnp.dot(disp_t[...], nb[c][q], preferred_element_type=F32).astype(BF16)
                out_b[c][:, q] = rows.reshape(E, CAP, B[c][1])
        to_experts(out_b[c], xb[c], db_send, db_recv.at[c, h], h)
        if h == 0:
            xb[c][0] = out_b[c][e]

    def direct_a(c, h):
        take(xa[c].at[z, others(h)], da_recv.at[c, h])
        rows = xa[c].at[z, half(h)]
        for i, zt in ((0, zp), (1, zm)):
            to_z(rows, rows, za_send, za_recv.at[0, c, h], zt).start()

    def forward_a(c, h):
        take(xa[c].at[pl.ds(0, 2), half(h)], za_recv.at[0, c, h])
        rows = xa[c].at[zm, pl.ds(h * EH, EQ)]
        to_z(rows, rows, za_send, za_recv.at[1, c, h], zp).start()
        rows = xa[c].at[zp, pl.ds(h * EH + EQ, EQ)]
        to_z(rows, rows, za_send, za_recv.at[1, c, h], zm).start()

    def multiply(blocks, at, h):
        base, width = at
        x = jnp.concatenate([b.reshape(SH, width) for b, _ in blocks], axis=1)
        for w_ref, acc in ((wg, acc_g), (wu, acc_u)):
            w = jnp.concatenate(
                [w_ref[pl.ds(pl.multiple_of(q * DZ + base, 128), width), :] for _, q in blocks], axis=0
            )
            acc[half_rows(h)] += jnp.dot(x, w, preferred_element_type=F32)

    def half_rows(h):
        return pl.ds(h * SH, SH)

    def multiply_near(c, h):
        multiply([(xa[c][q, half(h)], q) for q in (z, zp, zm)], A[c], h)

    def multiply_far(c, h):
        take(xa[c].at[zf, half(h)], za_recv.at[1, c, h])
        multiply([(xa[c][zf, half(h)], zf)], A[c], h)

    def multiply_b(c, h):
        take(xb[c].at[others(h)], db_recv.at[c, h])
        multiply([(xb[c][half(h), q], q) for q in range(NZ)], B[c], h)

    def wait_weights():
        take(wg, w_sem.at[0])
        take(wu, w_sem.at[1])

    def enter():
        pl.semaphore_wait(barrier, E - 1 + NZ - 1)

    def hidden(h):
        rows = half_rows(h)
        scale = scales[rows, 0:1]
        g = acc_g[rows] * scale
        hid[rows] = (g / (1.0 + jnp.exp(-g)) * (acc_u[rows] * scale)).astype(BF16)

    def wait_down():
        take(wd, w_sem.at[2])

    def down(q, at, h):
        lo, w = at
        ds = pl.ds(pl.multiple_of(q * DZ + lo, 128), w)
        return jnp.dot(hid[half_rows(h)], wd[:, ds], preferred_element_type=F32).astype(BF16)

    lo_t, hi_t = pl.ds(0, TH), pl.ds(TH, TH)

    def plus(a, b):
        return (a.astype(F32) + b.astype(F32)).astype(BF16)

    def quarters(h):
        return pl.ds(h * SH, SQ), pl.ds(h * SH + SQ, SQ)

    def far_part_a(c, h):
        lo, hi = quarters(h)
        far_a[c][half_rows(h)] = down(zf, A[c], h)
        to_z(far_a[c].at[lo], far_in_a[c].at[lo], ra_send, ra_recv.at[0, c, h], zp).start()
        to_z(far_a[c].at[hi], far_in_a[c].at[hi], ra_send, ra_recv.at[0, c, h], zm).start()

    def near_part_a(c, h):
        lo, hi = quarters(h)
        rows = half_rows(h)
        near_a[c][0, rows] = down(zp, A[c], h)
        near_a[c][1, rows] = down(zm, A[c], h)
        take(far_in_a[c].at[rows], ra_recv.at[0, c, h])
        near_a[c][0, lo] = plus(near_a[c][0, lo], far_in_a[c][lo])
        to_z(near_a[c].at[0, rows], near_in_a[c].at[0, rows], ra_send, ra_recv.at[1, c, h], zp).start()
        near_a[c][1, hi] = plus(near_a[c][1, hi], far_in_a[c][hi])
        to_z(near_a[c].at[1, rows], near_in_a[c].at[1, rows], ra_send, ra_recv.at[1, c, h], zm).start()

    def own_part_a(c, h):
        rows = half_rows(h)
        own = down(z, A[c], h).astype(F32)
        take(near_in_a[c].at[:, rows], ra_recv.at[1, c, h])
        own = own + near_in_a[c][0, rows].astype(F32) + near_in_a[c][1, rows].astype(F32)
        back_a[c][half(h)] = own.astype(BF16).reshape(EH, CAP, A[c][1])
        to_origins(back_a[c], ret_a[c], ya_send, ya_recv.at[c], h)
        if h == 0:
            ret_a[c][e] = back_a[c][0]

    def part_b(c, h):
        for q in range(NZ):
            back_b[c][half(h), q] = down(q, B[c], h).reshape(EH, CAP, B[c][1])
        to_origins(back_b[c], ret_b[c], yb_send, yb_recv.at[c], h)
        if h == 0:
            ret_b[c][e] = back_b[c][0]

    def weigh_b(c, q):
        return jnp.dot(comb[...], ret_b[c][:, q].reshape(S, B[c][1]), preferred_element_type=F32)

    def far_part_b(c):
        take(ret_b[c].at[rest], yb_recv.at[c])
        far_b[c][...] = weigh_b(c, zf).astype(BF16)
        to_z(far_b[c].at[lo_t], far_in_b[c].at[lo_t], rb_send, rb_recv.at[0, c], zp).start()
        to_z(far_b[c].at[hi_t], far_in_b[c].at[hi_t], rb_send, rb_recv.at[0, c], zm).start()

    def near_part_b(c):
        near_b[c][0] = weigh_b(c, zp).astype(BF16)
        near_b[c][1] = weigh_b(c, zm).astype(BF16)
        take(far_in_b[c], rb_recv.at[0, c])
        near_b[c][0, lo_t] = plus(near_b[c][0, lo_t], far_in_b[c][lo_t])
        to_z(near_b[c].at[0], near_in_b[c].at[0], rb_send, rb_recv.at[1, c], zp).start()
        near_b[c][1, hi_t] = plus(near_b[c][1, hi_t], far_in_b[c][hi_t])
        to_z(near_b[c].at[1], near_in_b[c].at[1], rb_send, rb_recv.at[1, c], zm).start()

    def own_part_b(c):
        own = weigh_b(c, z)
        take(near_in_b[c], rb_recv.at[1, c])
        own = own + near_in_b[c][0].astype(F32) + near_in_b[c][1].astype(F32)
        out_v[:, pl.ds(*B[c])] = own.astype(BF16)
        write_out(NA + c).start()

    def write_out(n):
        at = pl.ds(*(A + B)[n])
        return pltpu.make_async_copy(out_v.at[:, at], out_hbm.at[:, at], o_sem)

    def combine_a(c):
        take(ret_a[c].at[rest], ya_recv.at[c])
        got = jnp.dot(comb[...], ret_a[c][...].reshape(S, A[c][1]), preferred_element_type=F32)
        out_v[:, pl.ds(*A[c])] = got.astype(BF16)
        write_out(c).start()

    order = (
        (scale_b, 0), (scale_b, 1), (scale_b, 2), (enter,), (direct_b, 0), (dispatch_a, 0, 0), (direct_b, 1),
        (dispatch_a, 0, 1), (direct_b, 2), (dispatch_a, 1, 0), (dispatch_a, 1, 1), (squares,), (dispatch_a, 2, 0),
        (dispatch_a, 2, 1), (forward_b, 0), (dispatch_a, 3, 0), (dispatch_a, 3, 1), (prepare,), (forward_b, 1),
        (direct_a, 0, 0), (direct_a, 0, 1), (forward_b, 2), (send_scales,), (dispatch_b, 0, 0), (dispatch_b, 0, 1),
        (direct_a, 1, 0), (direct_a, 1, 1), (dispatch_b, 1, 0), (dispatch_b, 1, 1), (wait_weights,),
        (forward_a, 0, 0), (direct_a, 2, 0), (forward_a, 0, 1), (direct_a, 2, 1), (dispatch_b, 2, 0),
        (dispatch_b, 2, 1), (multiply_near, 0, 0), (multiply_near, 0, 1), (forward_a, 1, 0), (direct_a, 3, 0),
        (forward_a, 1, 1), (direct_a, 3, 1), (multiply_far, 0, 0), (multiply_far, 0, 1), (multiply_near, 1, 0),
        (multiply_near, 1, 1), (take_scales,), (multiply_b, 0, 0), (multiply_far, 1, 0), (multiply_b, 0, 1),
        (forward_a, 2, 0), (multiply_near, 2, 0), (forward_a, 2, 1), (multiply_far, 1, 1), (multiply_near, 2, 1),
        (multiply_b, 1, 0), (multiply_b, 1, 1), (forward_a, 3, 0), (multiply_near, 3, 0), (multiply_far, 2, 0),
        (multiply_far, 2, 1), (wait_down,), (forward_a, 3, 1), (multiply_b, 2, 0), (multiply_near, 3, 1),
        (multiply_far, 3, 0), (hidden, 0), (part_b, 1, 0), (far_part_a, 0, 0), (part_b, 0, 0), (far_part_a, 1, 0),
        (multiply_far, 3, 1), (multiply_b, 2, 1), (hidden, 1), (far_part_a, 0, 1), (part_b, 0, 1),
        (near_part_a, 0, 0), (far_part_a, 1, 1), (part_b, 1, 1), (near_part_a, 0, 1), (far_part_a, 2, 0),
        (near_part_a, 1, 0), (part_b, 2, 0), (far_part_a, 2, 1), (part_b, 2, 1), (near_part_a, 1, 1),
        (own_part_a, 0, 0), (far_part_a, 3, 0), (near_part_a, 2, 0), (own_part_a, 0, 1), (far_part_b, 0),
        (far_part_a, 3, 1), (near_part_a, 2, 1), (own_part_a, 1, 0), (own_part_a, 1, 1), (near_part_b, 0),
        (near_part_a, 3, 1), (own_part_a, 2, 0), (far_part_b, 1), (near_part_a, 3, 0), (far_part_b, 2),
        (own_part_a, 2, 1), (near_part_b, 1), (own_part_a, 3, 0), (near_part_b, 2), (combine_a, 0),
        (own_part_a, 3, 1), (own_part_b, 0), (combine_a, 1), (own_part_b, 1), (combine_a, 2), (own_part_b, 2),
        (combine_a, 3),
    )
    for step, *at in order:
        step(*at)

    take(out_v, o_sem)
    wa, wb = (sum(w for _, w in chunks) for chunks in (A, B))
    for sem, count in (
        (da_send, (S - CAP) * wa),
        (db_send, (S - CAP) * NZ * wb),
        (za_send, 3 * S * wa),
        (zb_send, 3 * T * wb),
        (ra_send, 3 * S * wa),
        (rb_send, 3 * T * wb),
        (ya_send, (S - CAP) * wa),
        (yb_send, (S - CAP) * NZ * wb),
    ):
        take(wg.at[pl.ds(0, count // wg.shape[1])], sem)
    take(sc_out.at[rest], sc_send)
    take(sq_buf.at[pl.ds(0, NZ - 1)], sq_send)


def local(cfg, tokens, norm_gain, expert_ids, gate_prob, w_gate, w_up, w_down):
    E, T, A, B = cfg["E"], cfg["T"], cfg["A"], cfg["B"]
    DZ, FFD = cfg["DZ"], cfg["FFD"]
    S = E * CAP
    hbm = pl.BlockSpec(memory_space=pl.ANY)
    TP = max(T, 128)
    dma = pltpu.SemaphoreType.DMA

    def each(chunks, *shape):
        return [pltpu.VMEM((*shape, w), BF16) for _, w in chunks]

    na, nb = len(A), len(B)
    scratch = [
        pltpu.VMEM((T, DZ), BF16),
        pltpu.VMEM((DZ,), BF16),
        pltpu.VMEM(expert_ids.shape[::-1], jnp.int32),
        pltpu.VMEM(expert_ids.shape[::-1], BF16),
        pltpu.VMEM((T, DZ), BF16),
        pltpu.VMEM((E, 1, 128), F32),
        pltpu.VMEM((E, 1, 128), F32),
        pltpu.VMEM((S, 128), F32),
        pltpu.VMEM((NZ * DZ, FFD), BF16),
        pltpu.VMEM((NZ * DZ, FFD), BF16),
        pltpu.VMEM((FFD, NZ * DZ), BF16),
        pltpu.VMEM((NZ, 8, TP), F32),
        pltpu.VMEM((S, T), BF16),
        pltpu.VMEM((T, S), BF16),
        pltpu.VMEM((S, FFD), F32),
        pltpu.VMEM((S, FFD), F32),
        pltpu.VMEM((S, FFD), BF16),
        dma((4,)),
        dma,
        dma((3,)),
        dma((10,)),
        dma((2,)),
        dma((1,)),
        [
            each(A, NZ, E, CAP),
            each(A, E, CAP),
            each(A, S),
            each(A, S),
            each(A, 2, S),
            each(A, 2, S),
            each(A, E, CAP),
            each(A, E, CAP),
        ],
        [
            each(B, E, NZ, CAP),
            each(B, NZ, T),
            each(B, E, NZ, CAP),
            each(B, E, NZ, CAP),
            each(B, E, NZ, CAP),
            each(B, T),
            each(B, T),
            each(B, 2, T),
            each(B, 2, T),
        ],
        [dma((na, 2)), dma((2, na, 2)), dma((2, na, 2)), dma((na,))],
        [dma((nb, 2)), dma((2, nb)), dma((2, nb)), dma((nb,))],
    ]
    return pl.pallas_call(
        functools.partial(moe_kernel, cfg),
        out_shape=jax.ShapeDtypeStruct((T, DZ), BF16),
        in_specs=[hbm] * 7,
        out_specs=hbm,
        scratch_shapes=scratch,
        compiler_params=pltpu.CompilerParams(
            collective_id=0, has_side_effects=True, vmem_limit_bytes=cfg["VMEM"]
        ),
        name="moe_layer",
    )(tokens, norm_gain, expert_ids.T, gate_prob.T, w_gate[0], w_up[0], w_down[0])


def config(mesh, tokens=8192, width=D, ff=2048, a=WIDTHS_A, b=WIDTHS_B, nx=4):
    E = mesh.shape["ep"]
    DZ = width // NZ
    chunks, lo = [], 0
    for w in (*a, *b):
        chunks.append((lo, w))
        lo += w
    assert lo == DZ
    return dict(
        E=E,
        T=tokens // E,
        D=width,
        DZ=DZ,
        FFD=ff // NZ,
        A=chunks[: len(a)],
        B=chunks[len(a) :],
        NX=nx,
        STRIDE=11,
        VMEM=67_000_000,
    )


def build(mesh, cfg):
    placed = (
        P("ep", "tp"),
        P("tp"),
        P("ep", None),
        P("ep", None),
        P("ep", None, "tp"),
        P("ep", None, "tp"),
        P("ep", "tp", None),
    )
    return jax.shard_map(
        functools.partial(local, cfg), mesh=mesh, in_specs=placed, out_specs=P("ep", "tp"), check_vma=False
    )


def solution(mesh):
    return build(mesh, config(mesh))
```

time: 116 us -> 112 us (0.966)
  Pallas kernels: 114 us -> 110 us
    pallas_call x1, Pallas kernels: 114 us -> 110 us  [local(): pl.pallas_call(functools.partial(moe_kernel, cfg), out_shape=jax.ShapeDty...]
where the time goes in v3:
time: 112 us
  Pallas kernels  110 us (98%)
  local copies, waits for them, and re-layouts  2.16 us (2%)
    pallas_call x1, Pallas kernels, local(): pl.pallas_call(functools.partial(moe_kernel, cfg), out_shape=jax.ShapeDty...  110 us

profile of v3, /device:TPU:1, one launch (start us, length us, event | category | flops | bytes accessed | tf_op | source)
XLA Modules:
  0.0 111.7 jit_solution(16237896796614199677)
XLA Ops:
  0.0 109.5 %moe_layer.1 = bf16[256,1792]{1,0:T(8,128)(2,1)} custom-call(bf16[256,1792]{1,0:T(8,128)(2,1)} %tokens_hbm.1, bf16[1792]{0:T(1024)(128)(2,1)} %gain_hbm.1, s32[8,256]{1,0:T(8,128)} %bitcast.8, bf16[8,256]{1,0:T(8,128)(2,1)} %bitcast.9, bf16[7168,512]{1,0:T(8,128)(2,1)} %bitcast.5, bf16[7168,512]{1,0:T(8,128)(2,1)} %bitcast.6, bf16[512,7168]{1,0:T(8,128)(2,1)} %bitcast.7), custom_call_target="tpu_custom_call" | custom-call | tf_op jit(solution)/shard_map/moe_layer/pallas_call | solution.py:521
  109.5 2.2 %copy.9 = bf16[256,1792]{1,0:T(8,128)(2,1)} copy(bf16[256,1792]{1,0:T(8,128)(2,1)} %moe_layer.1) | data formatting | bytes 1835008

commit v4 on v3

--- a/solution.py
+++ b/solution.py
@@ -424,8 +424,8 @@
         (dispatch_b, 2, 1), (multiply_near, 0, 0), (multiply_near, 0, 1), (forward_a, 1, 0), (direct_a, 3, 0),
         (forward_a, 1, 1), (direct_a, 3, 1), (multiply_far, 0, 0), (multiply_far, 0, 1), (multiply_near, 1, 0),
         (multiply_near, 1, 1), (take_scales,), (multiply_b, 0, 0), (multiply_far, 1, 0), (multiply_b, 0, 1),
-        (forward_a, 2, 0), (multiply_near, 2, 0), (forward_a, 2, 1), (multiply_far, 1, 1), (multiply_near, 2, 1),
-        (multiply_b, 1, 0), (multiply_b, 1, 1), (forward_a, 3, 0), (multiply_near, 3, 0), (multiply_far, 2, 0),
+        (forward_a, 2, 0), (multiply_far, 1, 1), (multiply_near, 2, 0), (forward_a, 2, 1), (multiply_near, 2, 1),
+        (forward_a, 3, 0), (multiply_b, 1, 0), (multiply_far, 2, 0), (multiply_b, 1, 1), (multiply_near, 3, 0),
         (multiply_far, 2, 1), (wait_down,), (forward_a, 3, 1), (multiply_b, 2, 0), (multiply_near, 3, 1),
         (multiply_far, 3, 0), (hidden, 0), (part_b, 1, 0), (far_part_a, 0, 0), (part_b, 0, 0), (far_part_a, 1, 0),
         (multiply_far, 3, 1), (multiply_b, 2, 1), (hidden, 1), (far_part_a, 0, 1), (part_b, 0, 1),
@@ -433,10 +433,9 @@
         (near_part_a, 1, 0), (part_b, 2, 0), (far_part_a, 2, 1), (part_b, 2, 1), (near_part_a, 1, 1),
         (own_part_a, 0, 0), (far_part_a, 3, 0), (near_part_a, 2, 0), (own_part_a, 0, 1), (far_part_b, 0),
         (far_part_a, 3, 1), (near_part_a, 2, 1), (own_part_a, 1, 0), (own_part_a, 1, 1), (near_part_b, 0),
-        (near_part_a, 3, 1), (own_part_a, 2, 0), (far_part_b, 1), (near_part_a, 3, 0), (far_part_b, 2),
-        (own_part_a, 2, 1), (near_part_b, 1), (own_part_a, 3, 0), (near_part_b, 2), (combine_a, 0),
-        (own_part_a, 3, 1), (own_part_b, 0), (combine_a, 1), (own_part_b, 1), (combine_a, 2), (own_part_b, 2),
-        (combine_a, 3),
+        (near_part_a, 3, 0), (own_part_a, 2, 0), (far_part_b, 1), (near_part_a, 3, 1), (own_part_a, 2, 1),
+        (own_part_a, 3, 0), (far_part_b, 2), (near_part_b, 1), (own_part_a, 3, 1), (near_part_b, 2), (combine_a, 0),
+        (own_part_b, 0), (combine_a, 1), (own_part_b, 1), (combine_a, 2), (own_part_b, 2), (combine_a, 3),
     )
     for step, *at in order:
         step(*at)

time: 112 us -> 111 us (level); the launches traced: 112 us -> 110 us
  Pallas kernels: 110 us -> 107 us
    pallas_call x1, Pallas kernels: 110 us -> 107 us  [local(): pl.pallas_call(functools.partial(moe_kernel, cfg), out_shape=jax.ShapeDty...]
where the time goes in v4:
time: 111 us; the launch traced here: 110 us
  Pallas kernels  107 us (96%)
  local copies, waits for them, and re-layouts  2.16 us (2%)
    pallas_call x1, Pallas kernels, local(): pl.pallas_call(functools.partial(moe_kernel, cfg), out_shape=jax.ShapeDty...  107 us

profile of v4, /device:TPU:1, one launch (start us, length us, event | category | flops | bytes accessed | tf_op | source)
XLA Modules:
  0.0 109.5 jit_solution(1489627915321695259)
XLA Ops:
  0.0 107.3 %moe_layer.1 = bf16[256,1792]{1,0:T(8,128)(2,1)} custom-call(bf16[256,1792]{1,0:T(8,128)(2,1)} %tokens_hbm.1, bf16[1792]{0:T(1024)(128)(2,1)} %gain_hbm.1, s32[8,256]{1,0:T(8,128)} %bitcast.8, bf16[8,256]{1,0:T(8,128)(2,1)} %bitcast.9, bf16[7168,512]{1,0:T(8,128)(2,1)} %bitcast.5, bf16[7168,512]{1,0:T(8,128)(2,1)} %bitcast.6, bf16[512,7168]{1,0:T(8,128)(2,1)} %bitcast.7), custom_call_target="tpu_custom_call" | custom-call | tf_op jit(solution)/shard_map/moe_layer/pallas_call | solution.py:520
  107.4 2.2 %copy.9 = bf16[256,1792]{1,0:T(8,128)(2,1)} copy(bf16[256,1792]{1,0:T(8,128)(2,1)} %moe_layer.1) | data formatting | bytes 1835008

commit v5 on v4

--- a/solution.py
+++ b/solution.py
@@ -204,10 +204,13 @@
         for i, zt in ((0, zp), (1, zm)):
             to_z(nb[c].at[z], nb[c].at[z], zb_send, zb_recv.at[0, c], zt).start()
 
+    def fill_a(c):
+        rows = jnp.dot(disp_t[...], scaled(A[c]), preferred_element_type=F32).astype(BF16)
+        out_a[c][...] = rows.reshape(E, CAP, A[c][1])
+
     def dispatch_a(c, h):
-        if h == 0:
-            rows = jnp.dot(disp_t[...], scaled(A[c]), preferred_element_type=F32).astype(BF16)
-            out_a[c][...] = rows.reshape(E, CAP, A[c][1])
+        if h == 0 and c > 1:
+            fill_a(c)
         to_experts(out_a[c], xa[c].at[z], da_send, da_recv.at[c, h], h)
         if h == 0:
             xa[c][z, 0] = out_a[c][e]
@@ -415,7 +418,7 @@
         write_out(c).start()
 
     order = (
-        (scale_b, 0), (scale_b, 1), (scale_b, 2), (enter,), (direct_b, 0), (dispatch_a, 0, 0), (direct_b, 1),
+        (scale_b, 0), (scale_b, 1), (scale_b, 2), (fill_a, 0), (fill_a, 1), (enter,), (direct_b, 0), (dispatch_a, 0, 0), (direct_b, 1),
         (dispatch_a, 0, 1), (direct_b, 2), (dispatch_a, 1, 0), (dispatch_a, 1, 1), (squares,), (dispatch_a, 2, 0),
         (dispatch_a, 2, 1), (forward_b, 0), (dispatch_a, 3, 0), (dispatch_a, 3, 1), (prepare,), (forward_b, 1),
         (direct_a, 0, 0), (direct_a, 0, 1), (forward_b, 2), (send_scales,), (dispatch_b, 0, 0), (dispatch_b, 0, 1),

time: 111 us -> 111 us (level)
  no operation moved by 1% of the time
where the time goes in v5:
time: 111 us; the launch traced here: 110 us
  Pallas kernels  107 us (96%)
  local copies, waits for them, and re-layouts  2.16 us (2%)
    pallas_call x1, Pallas kernels, local(): pl.pallas_call(functools.partial(moe_kernel, cfg), out_shape=jax.ShapeDty...  107 us

profile of v5, /device:TPU:1, one launch (start us, length us, event | category | flops | bytes accessed | tf_op | source)
XLA Modules:
  0.0 109.5 jit_solution(4005818709579186526)
XLA Ops:
  0.0 107.3 %moe_layer.1 = bf16[256,1792]{1,0:T(8,128)(2,1)} custom-call(bf16[256,1792]{1,0:T(8,128)(2,1)} %tokens_hbm.1, bf16[1792]{0:T(1024)(128)(2,1)} %gain_hbm.1, s32[8,256]{1,0:T(8,128)} %bitcast.8, bf16[8,256]{1,0:T(8,128)(2,1)} %bitcast.9, bf16[7168,512]{1,0:T(8,128)(2,1)} %bitcast.5, bf16[7168,512]{1,0:T(8,128)(2,1)} %bitcast.6, bf16[512,7168]{1,0:T(8,128)(2,1)} %bitcast.7), custom_call_target="tpu_custom_call" | custom-call | tf_op jit(solution)/shard_map/moe_layer/pallas_call | solution.py:523
  107.3 2.2 %copy.9 = bf16[256,1792]{1,0:T(8,128)(2,1)} copy(bf16[256,1792]{1,0:T(8,128)(2,1)} %moe_layer.1) | data formatting | bytes 1835008
